TPU v7x, 256 devices: a whole 4x4x8 slice. The times are simulated.
256 devices in a mesh: row: 32 (over y, x, core), col: 8 (over z).
Axes of the slice: x: 4, y: 4, z: 8, core: 2. Of those that a mesh axis runs over, the one named last changes fastest.
Arguments:
- sources: float32 [3, 4096, 8192], P(None, 'row', 'col'), may hold values from -32 to 32
- labels: int32 [4096, 8192], P('row', 'col'), may hold values from 0 to 2
Outputs:
- blended: float32 [4096, 8192], P('row', 'col')
- overview_fine: float32 [2048, 4096], P('row', 'col')
- overview_mid: float32 [1024, 2048], P(None, 'col')
- overview_coarse: float32 [512, 1024], P(None, 'col')
All inputs are finite; a program needn't handle non-finite values.
Results may differ from a plain program's by a relative error of at most 0.0001.
Values sent between devices are 32-bit elements; how exact they have to be, the bound alone decides.
A program may use at most 64 MiB of HBM per device.

v0:
```python
import jax
import jax.numpy as jnp
from jax import lax
from jax.sharding import Mesh
from jax.sharding import PartitionSpec as P

ITERS = 3
ROW_COL = ("row_0", "row_1", "row_2", "col")
ROW = ("row_0", "row_1", "row_2")


def padded_2(value, sides, width):
    edges = {}
    for axis, dim in sides:
        devices, length = (lax.axis_size(axis), value.shape[dim])
        up = [(i, (i + 1) % devices) for i in range(devices - 1)]
        last = lax.slice_in_dim(value, length - width, length, axis=dim)
        leading = lax.slice_in_dim(value, 0, width, axis=dim)
        edges[dim] = (
            lax.ppermute(last, axis, up),
            lax.ppermute(leading, axis, [(b, a) for a, b in up]),
        )
    done = []
    for _, dim in sides:
        low, high = edges[dim]
        around = [(width, width) if d in done else (0, 0) for d in range(value.ndim)]
        value = jnp.concatenate([jnp.pad(low, around), value, jnp.pad(high, around)], axis=dim)
        done.append(dim)
    return value


def by_axis(value, axes):
    for axis in axes:
        value = lax.psum(value, axis)
    return value


def from_everyone(value, axis):
    copies = jnp.broadcast_to(value, (lax.axis_size(axis), *value.shape))
    return lax.all_to_all(copies, axis, split_axis=0, concat_axis=0, tiled=True)


def laid_out(tiles, dim):
    tiles = jnp.moveaxis(tiles, 0, dim)
    dims = tiles.shape
    return tiles.reshape(*dims[:dim], dims[dim] * dims[dim + 1], *dims[dim + 2 :])


def gathered_copies(value, axis, dim):
    tiles = from_everyone(value, axis)
    return laid_out(tiles, dim)


def stencil_padded(padded, values):
    beside = padded[2:, 1:-1] + padded[:-2, 1:-1]
    beside = beside + padded[1:-1, 2:] + padded[1:-1, :-2]
    return 4.0 * values - beside


def apply_stencil(values):
    padded = padded_2(values, ((ROW, 0), ("col", 1)), 1)
    return stencil_padded(padded, values)


def average_pool(values):
    return 0.25 * (
        values[0::2, 0::2] + values[1::2, 0::2] + values[0::2, 1::2] + values[1::2, 1::2]
    )


def two_products(residual, applied):
    return (
        by_axis(jnp.sum(residual * residual), ROW_COL),
        by_axis(jnp.sum(residual * applied), ROW_COL),
    )


def per_device(sources, labels):
    source_pad = padded_2(sources, ((ROW, 1), ("col", 2)), 1)
    right_side = jnp.zeros(labels.shape, jnp.float32)
    for channel in range(sources.shape[0]):
        stencil_term = stencil_padded(source_pad[channel], sources[channel])
        right_side = right_side + jnp.where(labels == channel, stencil_term, jnp.float32(0.0))
    blended = jnp.zeros(labels.shape, jnp.float32)
    residual = right_side
    applied = apply_stencil(residual)
    norm_now, product = two_products(residual, applied)
    step_size = norm_now / product
    direction = residual
    along = applied
    for iteration in range(ITERS):
        blended = blended + step_size * direction
        residual = residual - step_size * along
        if iteration + 1 < ITERS:
            applied = apply_stencil(residual)
            norm_next, product = two_products(residual, applied)
            beta_ratio = norm_next / norm_now
            step_size = norm_next / (product - beta_ratio * norm_next / step_size)
            direction = residual + beta_ratio * direction
            along = applied + beta_ratio * along
            norm_now = norm_next
    overview_fine = average_pool(blended)
    overview_mid = gathered_copies(average_pool(overview_fine), ROW, 0)
    overview_coarse = average_pool(overview_mid)
    return (blended, overview_fine, overview_mid, overview_coarse)


def solution(mesh):
    finer = Mesh(
        mesh.devices.reshape(4, 4, 2, mesh.shape["col"]), ("row_0", "row_1", "row_2", "col")
    )
    return jax.shard_map(
        per_device,
        mesh=finer,
        in_specs=(P(None, ROW, "col"), P(ROW, "col")),
        out_specs=(P(ROW, "col"), P(ROW, "col"), P(None, "col"), P(None, "col")),
        check_vma=False,
    )
```

profile of v0, /device:TPU:1, one launch (start us, length us, event | category | flops | bytes accessed | tf_op | source)
XLA Modules:
  0.0 306.4 jit_solution(11265011908296794969)
XLA Ops:
  33.5 4.7 %collective-permute-start.7 = (f32[128,1]{1,0:T(8,128)S(1)}, f32[128,1]{1,0:T(8,128)S(1)}, u32[]{:S(2)}, u32[]{:S(2)}) collective-permute-start(f32[128,1]{1,0:T(8,128)S(1)} %get-tuple-element.50), channel_id=1, source_target_pairs={{0,1},{1,2},{2,3},{3,4},{4,5},{5,6},{6,7},{8,9},{9,10},{10,11},{11... | collective-permute-start | bytes 1544 | tf_op jit(solution)/shard_map/ppermute | solution.py:20
  40.6 9.4 %all-reduce.16 = (f32[]{:T(128)}, f32[]{:T(128)}) all-reduce(f32[]{:T(128)} %get-tuple-element.9, f32[]{:T(128)} %get-tuple-element.8), channel_id=1, replica_groups=mesh['row_0'=4,'row_1'=4,'row_2'=2,'col'=8] {'row_0'}, use_global_device_ids=true, to_apply=%region_1.2 | all-reduce | flops 2 | bytes 16 | tf_op jit(solution)/shard_map/psum | solution.py:34
  50.0 9.3 %all-reduce.13 = (f32[]{:T(128)}, f32[]{:T(128)}) all-reduce(f32[]{:T(128)} %get-tuple-element.26, f32[]{:T(128)} %get-tuple-element.27), channel_id=1, replica_groups=mesh['row_0'=4,'row_1'=4,'row_2'=2,'col'=8] {'row_1'}, use_global_device_ids=true, to_apply=%region_2.3 | all-reduce | flops 2 | bytes 16 | tf_op jit(solution)/shard_map/psum | solution.py:34
  59.3 8.5 %all-reduce.19 = (f32[]{:T(128)}, f32[]{:T(128)}) all-reduce(f32[]{:T(128)} %get-tuple-element.20, f32[]{:T(128)} %get-tuple-element.21), channel_id=1, replica_groups=mesh['row_0'=4,'row_1'=4,'row_2'=2,'col'=8] {'row_2'}, use_global_device_ids=true, to_apply=%region_3.4 | all-reduce | flops 2 | bytes 16 | tf_op jit(solution)/shard_map/psum | solution.py:34
  67.8 19.2 %all-reduce.10 = (f32[]{:T(128)}, f32[]{:T(128)}) all-reduce(f32[]{:T(128)} %get-tuple-element.32, f32[]{:T(128)} %get-tuple-element.33), channel_id=1, replica_groups=mesh['row_0'=4,'row_1'=4,'row_2'=2,'col'=8] {'col'}, use_global_device_ids=true, to_apply=%region_4.5 | all-reduce | flops 2 | bytes 16 | tf_op jit(solution)/shard_map/psum | solution.py:34
  88.7 7.6 %collective-permute-start.9 = (f32[1,1024]{1,0:T(1,128)S(1)}, f32[1,1024]{1,0:T(1,128)S(1)}, u32[]{:S(2)}, u32[]{:S(2)}) collective-permute-start(f32[1,1024]{1,0:T(1,128)S(1)} %get-tuple-element.47), channel_id=1, source_target_pairs={{0,8},{8,16},{16,24},{24,32},{32,40},{40,48},{48,56},{56,64},{64,7... | collective-permute-start | bytes 12296 | tf_op jit(solution)/shard_map/ppermute | solution.py:20
  106.0 6.6 %all-reduce.15 = (f32[]{:T(128)}, f32[]{:T(128)}) all-reduce(f32[]{:T(128)} %get-tuple-element.7, f32[]{:T(128)} %get-tuple-element.6), channel_id=1, replica_groups=mesh['row_0'=4,'row_1'=4,'row_2'=2,'col'=8] {'row_0'}, use_global_device_ids=true, to_apply=%region_11.12 | all-reduce | flops 2 | bytes 16 | tf_op jit(solution)/shard_map/psum | solution.py:34
  112.6 7.5 %all-reduce.12 = (f32[]{:T(128)}, f32[]{:T(128)}) all-reduce(f32[]{:T(128)} %get-tuple-element.24, f32[]{:T(128)} %get-tuple-element.25), channel_id=1, replica_groups=mesh['row_0'=4,'row_1'=4,'row_2'=2,'col'=8] {'row_1'}, use_global_device_ids=true, to_apply=%region_12.13 | all-reduce | flops 2 | bytes 16 | tf_op jit(solution)/shard_map/psum | solution.py:34
  120.1 8.6 %all-reduce.18 = (f32[]{:T(128)}, f32[]{:T(128)}) all-reduce(f32[]{:T(128)} %get-tuple-element.18, f32[]{:T(128)} %get-tuple-element.19), channel_id=1, replica_groups=mesh['row_0'=4,'row_1'=4,'row_2'=2,'col'=8] {'row_2'}, use_global_device_ids=true, to_apply=%region_13.14 | all-reduce | flops 2 | bytes 16 | tf_op jit(solution)/shard_map/psum | solution.py:34
  128.7 13.4 %all-reduce.9 = (f32[]{:T(128)}, f32[]{:T(128)}) all-reduce(f32[]{:T(128)} %get-tuple-element.30, f32[]{:T(128)} %get-tuple-element.31), channel_id=1, replica_groups=mesh['row_0'=4,'row_1'=4,'row_2'=2,'col'=8] {'col'}, use_global_device_ids=true, to_apply=%region_14.15 | all-reduce | flops 2 | bytes 16 | tf_op jit(solution)/shard_map/psum | solution.py:34
  147.4 7.5 %collective-permute-start.13 = (f32[1,1024]{1,0:T(1,128)S(1)}, f32[1,1024]{1,0:T(1,128)S(1)}, u32[]{:S(2)}, u32[]{:S(2)}) collective-permute-start(f32[1,1024]{1,0:T(1,128)S(1)} %get-tuple-element.43), channel_id=1, source_target_pairs={{0,8},{8,16},{16,24},{24,32},{32,40},{40,48},{48,56},{56,64},{64,7... | collective-permute-start | bytes 12296 | tf_op jit(solution)/shard_map/ppermute | solution.py:20
  164.4 6.9 %all-reduce.14 = (f32[]{:T(128)}, f32[]{:T(128)}) all-reduce(f32[]{:T(128)} %get-tuple-element.5, f32[]{:T(128)} %get-tuple-element.4), channel_id=1, replica_groups=mesh['row_0'=4,'row_1'=4,'row_2'=2,'col'=8] {'row_0'}, use_global_device_ids=true, to_apply=%region_21.22 | all-reduce | flops 2 | bytes 16 | tf_op jit(solution)/shard_map/psum | solution.py:34
  171.3 9.6 %all-reduce.11 = (f32[]{:T(128)}, f32[]{:T(128)}) all-reduce(f32[]{:T(128)} %get-tuple-element.22, f32[]{:T(128)} %get-tuple-element.23), channel_id=1, replica_groups=mesh['row_0'=4,'row_1'=4,'row_2'=2,'col'=8] {'row_1'}, use_global_device_ids=true, to_apply=%region_22.23 | all-reduce | flops 2 | bytes 16 | tf_op jit(solution)/shard_map/psum | solution.py:34
  180.9 8.5 %all-reduce.17 = (f32[]{:T(128)}, f32[]{:T(128)}) all-reduce(f32[]{:T(128)} %get-tuple-element.16, f32[]{:T(128)} %get-tuple-element.17), channel_id=1, replica_groups=mesh['row_0'=4,'row_1'=4,'row_2'=2,'col'=8] {'row_2'}, use_global_device_ids=true, to_apply=%region_23.24 | all-reduce | flops 2 | bytes 16 | tf_op jit(solution)/shard_map/psum | solution.py:34
  189.4 14.3 %all-reduce.8 = (f32[]{:T(128)}, f32[]{:T(128)}) all-reduce(f32[]{:T(128)} %get-tuple-element.28, f32[]{:T(128)} %get-tuple-element.29), channel_id=1, replica_groups=mesh['row_0'=4,'row_1'=4,'row_2'=2,'col'=8] {'col'}, use_global_device_ids=true, to_apply=%region_24.25 | all-reduce | flops 2 | bytes 16 | tf_op jit(solution)/shard_map/psum | solution.py:34
  208.6 4.5 %slice.235 = f32[64,512]{1,0:T(8,128)S(1)} slice(f32[128,1024]{1,0:T(8,128)S(1)} %multiply_add_fusion), slice={[1:128:2], [1:1024:2]} | slice | bytes 262144 | tf_op jit(solution)/shard_map/slice | solution.py:67
  213.1 4.5 %slice.234 = f32[64,512]{1,0:T(8,128)S(1)} slice(f32[128,1024]{1,0:T(8,128)S(1)} %multiply_add_fusion), slice={[0:128:2], [1:1024:2]} | slice | bytes 262144 | tf_op jit(solution)/shard_map/slice | solution.py:67
  217.6 4.5 %slice.233 = f32[64,512]{1,0:T(8,128)S(1)} slice(f32[128,1024]{1,0:T(8,128)S(1)} %multiply_add_fusion), slice={[1:128:2], [0:1024:2]} | slice | bytes 262144 | tf_op jit(solution)/shard_map/slice | solution.py:67
  222.1 4.7 %slice.232 = f32[64,512]{1,0:T(8,128)S(1)} slice(f32[128,1024]{1,0:T(8,128)S(1)} %multiply_add_fusion), slice={[0:128:2], [0:1024:2]} | slice | bytes 262144 | tf_op jit(solution)/shard_map/slice | solution.py:67
  231.7 24.6 %all_to_all.5 = f32[32,32,256]{2,1,0:T(8,128)S(1)} all-to-all(f32[32,32,256]{2,1,0:T(8,128)S(1)} %broadcast_in_dim.10), channel_id=1, replica_groups=mesh['row_0'=4,'row_1'=4,'row_2'=2,'col'=8] {'row_0','row_1','row_2'}, dimensions={0} | all-to-all | bytes 2097152 | tf_op jit(solution)/shard_map/all_to_all | solution.py:40
  256.3 12.0 %slice.243 = f32[512,128]{1,0:T(8,128)S(1)} slice(f32[1024,256]{1,0:T(8,128)S(1)} %bitcast.13), slice={[1:1024:2], [1:256:2]} | slice | bytes 524288 | tf_op jit(solution)/shard_map/slice | solution.py:67
  268.3 12.0 %slice.242 = f32[512,128]{1,0:T(8,128)S(1)} slice(f32[1024,256]{1,0:T(8,128)S(1)} %bitcast.14), slice={[0:1024:2], [1:256:2]} | slice | bytes 524288 | tf_op jit(solution)/shard_map/slice | solution.py:67
  280.3 12.0 %slice.241 = f32[512,128]{1,0:T(8,128)S(1)} slice(f32[1024,256]{1,0:T(8,128)S(1)} %bitcast.15), slice={[1:1024:2], [0:256:2]} | slice | bytes 524288 | tf_op jit(solution)/shard_map/slice | solution.py:67
  292.3 12.3 %slice.240 = f32[512,128]{1,0:T(8,128)S(1)} slice(f32[1024,256]{1,0:T(8,128)S(1)} %bitcast.16), slice={[0:1024:2], [0:256:2]} | slice | bytes 524288 | tf_op jit(solution)/shard_map/slice | solution.py:67
  (66 shorter events, 62.6 us)
Async XLA Ops:
  0.6 18.9 %copy-start = (f32[3,128,1024]{2,1,0:T(8,128)S(1)}, f32[3,128,1024]{2,1,0:T(8,128)}, u32[]{:S(2)}) copy-start(f32[3,128,1024]{2,1,0:T(8,128)} %param.2) | copy-start | bytes 4718596
  1.7 17.8 %collective-permute-start.1 = (f32[3,1,1024]{2,1,0:T(1,128)S(1)}, f32[3,1,1024]{2,1,0:T(1,128)S(1)}, u32[]{:S(2)}, u32[]{:S(2)}) collective-permute-start(f32[3,1,1024]{2,1,0:T(1,128)S(1)} %get-tuple-element.39), channel_id=1, source_target_pairs={{0,8},{8,16},{16,24},{24,32},{32,40},{40,48},{48,56},{56,64},{64,7... | collective-permute-start | bytes 36872 | tf_op jit(solution)/shard_map/ppermute | solution.py:20
  6.2 13.3 %collective-permute-start.2 = (f32[3,1,1024]{2,1,0:T(1,128)S(1)}, f32[3,1,1024]{2,1,0:T(1,128)S(1)}, u32[]{:S(2)}, u32[]{:S(2)}) collective-permute-start(f32[3,1,1024]{2,1,0:T(1,128)S(1)} %get-tuple-element.40), channel_id=1, source_target_pairs={{8,0},{16,8},{24,16},{32,24},{40,32},{48,40},{56,48},{64,56},{72,6... | collective-permute-start | bytes 36872 | tf_op jit(solution)/shard_map/ppermute | solution.py:21
  9.3 8.3 %collective-permute-start.3 = (f32[3,128,1]{2,1,0:T(8,128)S(1)}, f32[3,128,1]{2,1,0:T(8,128)S(1)}, u32[]{:S(2)}, u32[]{:S(2)}) collective-permute-start(f32[3,128,1]{2,1,0:T(8,128)S(1)} %get-tuple-element.37), channel_id=1, source_target_pairs={{1,0},{2,1},{3,2},{4,3},{5,4},{6,5},{7,6},{9,8},{10,9},{11,10},{12... | collective-permute-start | bytes 4616 | tf_op jit(solution)/shard_map/ppermute | solution.py:21
  10.6 8.9 %collective-permute-start = (f32[3,128,1]{2,1,0:T(8,128)S(1)}, f32[3,128,1]{2,1,0:T(8,128)S(1)}, u32[]{:S(2)}, u32[]{:S(2)}) collective-permute-start(f32[3,128,1]{2,1,0:T(8,128)S(1)} %get-tuple-element.38), channel_id=1, source_target_pairs={{0,1},{1,2},{2,3},{3,4},{4,5},{5,6},{6,7},{8,9},{9,10},{10,11},{11... | collective-permute-start | bytes 4616 | tf_op jit(solution)/shard_map/ppermute | solution.py:20
  23.7 1.6 copy-start.2
  26.8 12.8 %collective-permute-start.5 = (f32[1,1024]{1,0:T(1,128)S(1)}, f32[1,1024]{1,0:T(1,128)S(1)}, u32[]{:S(2)}, u32[]{:S(2)}) collective-permute-start(f32[1,1024]{1,0:T(1,128)S(1)} %get-tuple-element.51), channel_id=1, source_target_pairs={{0,8},{8,16},{16,24},{24,32},{32,40},{40,48},{48,56},{56,64},{64,7... | collective-permute-start | bytes 12296 | tf_op jit(solution)/shard_map/ppermute | solution.py:20
  30.2 9.4 %collective-permute-start.4 = (f32[1,1024]{1,0:T(1,128)S(1)}, f32[1,1024]{1,0:T(1,128)S(1)}, u32[]{:S(2)}, u32[]{:S(2)}) collective-permute-start(f32[1,1024]{1,0:T(1,128)S(1)} %get-tuple-element.52), channel_id=1, source_target_pairs={{8,0},{16,8},{24,16},{32,24},{40,32},{48,40},{56,48},{64,56},{72,6... | collective-permute-start | bytes 12296 | tf_op jit(solution)/shard_map/ppermute | solution.py:21
  32.2 6.0 %collective-permute-start.6 = (f32[128,1]{1,0:T(8,128)S(1)}, f32[128,1]{1,0:T(8,128)S(1)}, u32[]{:S(2)}, u32[]{:S(2)}) collective-permute-start(f32[128,1]{1,0:T(8,128)S(1)} %get-tuple-element.49), channel_id=1, source_target_pairs={{1,0},{2,1},{3,2},{4,3},{5,4},{6,5},{7,6},{9,8},{10,9},{11,10},{12... | collective-permute-start | bytes 1544 | tf_op jit(solution)/shard_map/ppermute | solution.py:21
  33.5 6.1 %collective-permute-start.7 = (f32[128,1]{1,0:T(8,128)S(1)}, f32[128,1]{1,0:T(8,128)S(1)}, u32[]{:S(2)}, u32[]{:S(2)}) collective-permute-start(f32[128,1]{1,0:T(8,128)S(1)} %get-tuple-element.50), channel_id=1, source_target_pairs={{0,1},{1,2},{2,3},{3,4},{4,5},{5,6},{6,7},{8,9},{9,10},{10,11},{11... | collective-permute-start | bytes 1544 | tf_op jit(solution)/shard_map/ppermute | solution.py:20
  88.7 16.2 %collective-permute-start.9 = (f32[1,1024]{1,0:T(1,128)S(1)}, f32[1,1024]{1,0:T(1,128)S(1)}, u32[]{:S(2)}, u32[]{:S(2)}) collective-permute-start(f32[1,1024]{1,0:T(1,128)S(1)} %get-tuple-element.47), channel_id=1, source_target_pairs={{0,8},{8,16},{16,24},{24,32},{32,40},{40,48},{48,56},{56,64},{64,7... | collective-permute-start | bytes 12296 | tf_op jit(solution)/shard_map/ppermute | solution.py:20
  96.4 8.6 %collective-permute-start.8 = (f32[1,1024]{1,0:T(1,128)S(1)}, f32[1,1024]{1,0:T(1,128)S(1)}, u32[]{:S(2)}, u32[]{:S(2)}) collective-permute-start(f32[1,1024]{1,0:T(1,128)S(1)} %get-tuple-element.48), channel_id=1, source_target_pairs={{8,0},{16,8},{24,16},{32,24},{40,32},{48,40},{56,48},{64,56},{72,6... | collective-permute-start | bytes 12296 | tf_op jit(solution)/shard_map/ppermute | solution.py:21
  98.4 5.3 %collective-permute-start.10 = (f32[128,1]{1,0:T(8,128)S(1)}, f32[128,1]{1,0:T(8,128)S(1)}, u32[]{:S(2)}, u32[]{:S(2)}) collective-permute-start(f32[128,1]{1,0:T(8,128)S(1)} %get-tuple-element.45), channel_id=1, source_target_pairs={{1,0},{2,1},{3,2},{4,3},{5,4},{6,5},{7,6},{9,8},{10,9},{11,10},{12... | collective-permute-start | bytes 1544 | tf_op jit(solution)/shard_map/ppermute | solution.py:21
  99.7 5.3 %collective-permute-start.11 = (f32[128,1]{1,0:T(8,128)S(1)}, f32[128,1]{1,0:T(8,128)S(1)}, u32[]{:S(2)}, u32[]{:S(2)}) collective-permute-start(f32[128,1]{1,0:T(8,128)S(1)} %get-tuple-element.46), channel_id=1, source_target_pairs={{0,1},{1,2},{2,3},{3,4},{4,5},{5,6},{6,7},{8,9},{9,10},{10,11},{11... | collective-permute-start | bytes 1544 | tf_op jit(solution)/shard_map/ppermute | solution.py:20
  147.4 16.1 %collective-permute-start.13 = (f32[1,1024]{1,0:T(1,128)S(1)}, f32[1,1024]{1,0:T(1,128)S(1)}, u32[]{:S(2)}, u32[]{:S(2)}) collective-permute-start(f32[1,1024]{1,0:T(1,128)S(1)} %get-tuple-element.43), channel_id=1, source_target_pairs={{0,8},{8,16},{16,24},{24,32},{32,40},{40,48},{48,56},{56,64},{64,7... | collective-permute-start | bytes 12296 | tf_op jit(solution)/shard_map/ppermute | solution.py:20
  154.8 8.6 %collective-permute-start.12 = (f32[1,1024]{1,0:T(1,128)S(1)}, f32[1,1024]{1,0:T(1,128)S(1)}, u32[]{:S(2)}, u32[]{:S(2)}) collective-permute-start(f32[1,1024]{1,0:T(1,128)S(1)} %get-tuple-element.44), channel_id=1, source_target_pairs={{8,0},{16,8},{24,16},{32,24},{40,32},{48,40},{56,48},{64,56},{72,6... | collective-permute-start | bytes 12296 | tf_op jit(solution)/shard_map/ppermute | solution.py:21
  156.8 5.3 %collective-permute-start.14 = (f32[128,1]{1,0:T(8,128)S(1)}, f32[128,1]{1,0:T(8,128)S(1)}, u32[]{:S(2)}, u32[]{:S(2)}) collective-permute-start(f32[128,1]{1,0:T(8,128)S(1)} %get-tuple-element.41), channel_id=1, source_target_pairs={{1,0},{2,1},{3,2},{4,3},{5,4},{6,5},{7,6},{9,8},{10,9},{11,10},{12... | collective-permute-start | bytes 1544 | tf_op jit(solution)/shard_map/ppermute | solution.py:21
  158.1 5.3 %collective-permute-start.15 = (f32[128,1]{1,0:T(8,128)S(1)}, f32[128,1]{1,0:T(8,128)S(1)}, u32[]{:S(2)}, u32[]{:S(2)}) collective-permute-start(f32[128,1]{1,0:T(8,128)S(1)} %get-tuple-element.42), channel_id=1, source_target_pairs={{0,1},{1,2},{2,3},{3,4},{4,5},{5,6},{6,7},{8,9},{9,10},{10,11},{11... | collective-permute-start | bytes 1544 | tf_op jit(solution)/shard_map/ppermute | solution.py:20
  208.5 47.8 %copy-start.1 = (f32[128,1024]{1,0:T(8,128)}, f32[128,1024]{1,0:T(8,128)S(1)}, u32[]{:S(2)}) copy-start(f32[128,1024]{1,0:T(8,128)S(1)} %multiply_add_fusion) | copy-start | bytes 1572868
  226.9 29.4 %copy-start.3 = (f32[64,512]{1,0:T(8,128)}, f32[64,512]{1,0:T(8,128)S(1)}, u32[]{:S(2)}) copy-start(f32[64,512]{1,0:T(8,128)S(1)} %add_multiply_fusion.1) | copy-start | bytes 393220
where the time goes:
time: 307 us; the launch traced here: 306 us
  blocking collectives  146 us (48%)
  local copies, waits for them, and re-layouts  79.2 us (26%)
  starting transfers between devices  52.7 us (17%)
  between operations  11 us (4%)
  waiting for transfers between devices  8.59 us (3%)
  other arithmetic  8.45 us (3%)
    psum x12, blocking collectives, by_axis(): value = lax.psum(value, axis)  122 us
    ppermute x8, starting transfers between devices, padded_2(): lax.ppermute(last, axis, up)  39.9 us
    all_to_all x1, blocking collectives, from_everyone(): return lax.all_to_all(copies, axis, split_axis=0, concat_axis=0, tiled=True)  24.6 us
    slice x3, local copies, waits for them, and re-layouts, average_pool(): values[0::2, 0::2] + values[1::2, 0::2] + values[0::2, 1::2]  18.2 us
    slice x3, local copies, waits for them, and re-layouts, average_pool(): values[1::2, 0::2]  17.7 us
    slice x3, local copies, waits for them, and re-layouts, average_pool(): values[0::2, 1::2]  17.7 us
    slice x3, local copies, waits for them, and re-layouts, average_pool(): values[1::2, 1::2]  17.7 us
    ppermute x8, starting transfers between devices, padded_2(): lax.ppermute(leading, axis, [(b, a) for a, b in up])  12.8 us
  transfers between devices with their start and end apart: 16, of which 5 were waited for; matrix products, arithmetic and copies ran while one was open for 0% of the time, Pallas kernels for 0%

commit v1 on v0

v1 whole, which is shorter than its diff:
```python
import jax
import jax.numpy as jnp
from jax import lax
from jax.experimental import pallas as pl
from jax.experimental.pallas import tpu as pltpu
from jax.sharding import PartitionSpec as P

MESH = pl.DeviceIdType.MESH
F32 = jnp.float32
T = 8
ROWS = 144
LANE_ROLL = 127


def two_sum(a, b):
    s = a + b
    t = s - a
    return s, (a - (s - t)) + (b - t)


def dd_add(a, b):
    s, e = two_sum(a[0], b[0])
    return two_sum(s, e + (a[1] + b[1]))


def dd_neg(a):
    return (-a[0], -a[1])


def dd_sub(a, b):
    return dd_add(a, dd_neg(b))


def split(a):
    t = a * 4097.0
    hi = t - (t - a)
    return hi, a - hi


def two_prod(a, b):
    p = a * b
    ah, al = split(a)
    bh, bl = split(b)
    return p, ((ah * bh - p) + ah * bl + al * bh) + al * bl


def dd_mul(a, b):
    p, e = two_prod(a[0], b[0])
    return two_sum(p, e + (a[0] * b[1] + a[1] * b[0]))


def dd_div(a, b):
    q = a[0] / b[0]
    p, e = two_prod(q, b[0])
    r = ((a[0] - p) - e) + (a[1] - q * b[1])
    return two_sum(q, r / b[0])


def krylov_weights(n):
    l1 = dd_div(n[2], n[1])
    l2 = dd_div(n[3], n[1])
    d1 = dd_sub(n[3], dd_mul(l1, n[2]))
    e = dd_sub(n[4], dd_mul(l1, n[3]))
    l3 = dd_div(e, d1)
    d2 = dd_sub(dd_sub(n[5], dd_mul(l2, n[3])), dd_mul(l3, e))
    y1 = dd_sub(n[1], dd_mul(l1, n[0]))
    y2 = dd_sub(dd_sub(n[2], dd_mul(l2, n[0])), dd_mul(l3, y1))
    ok1 = d1[0] > 1e-10 * n[3][0]
    ok2 = ok1 & (d2[0] > 1e-10 * n[5][0])
    c2 = tuple(jnp.where(ok2, v, 0.0) for v in dd_div(y2, d2))
    c1 = dd_sub(dd_div(y1, d1), dd_mul(l3, c2))
    c1 = tuple(jnp.where(ok1, v, 0.0) for v in c1)
    c0 = dd_sub(dd_sub(dd_div(n[0], n[1]), dd_mul(l1, c1)), dd_mul(l2, c2))
    return c0[0], c1[0], c2[0]


def pool_lanes(pair):
    src = lax.broadcasted_iota(jnp.int32, (256, 128), 0)
    dst = lax.broadcasted_iota(jnp.int32, (256, 128), 1)
    weight = jnp.where(src // 2 == dst, 0.25, 0.0).astype(jnp.bfloat16)
    hi = pair.astype(jnp.bfloat16)
    rest = pair - hi.astype(F32)
    mid = rest.astype(jnp.bfloat16)
    low = (rest - mid.astype(F32)).astype(jnp.bfloat16)
    dot = lambda v: jnp.dot(v, weight, preferred_element_type=F32)
    return dot(hi) + dot(mid) + dot(low)


def make_kernel(n_row, n_col):
    n_chip = n_row // 2

    def kernel(src, lab, o_blend, o_fine, o_mid, o_coarse,
               E, L, V, O, FI, GM, CO, strip, strip_in, corner_in, corner_lab,
               msg, red_row, red_col,
               load_sem, halo_send, halo_recv, red_send, red_recv,
               g_send, g_recv, out_sem):
        row = lax.axis_index("row")
        col = lax.axis_index("col")
        has_up, has_down = row > 0, row < n_row - 1
        has_left, has_right = col > 0, col < n_col - 1

        loads = []
        for j in range(T):
            lanes = pl.ds(128 * j, 128)
            loads.append(pltpu.make_async_copy(
                src.at[:, :, lanes], E.at[:, j, pl.ds(8, 128), :], load_sem.at[2 * j]))
            loads.append(pltpu.make_async_copy(
                lab.at[:, lanes], L.at[j, pl.ds(8, 128), :], load_sem.at[2 * j + 1]))
        for cp in loads:
            cp.start()

        barrier = pltpu.get_barrier_semaphore()

        @pl.loop(1, n_row)
        def _(i):
            pl.semaphore_signal(barrier, inc=1, device_id={"row": (row + i) % n_row, "col": col},
                                device_id_type=MESH)

        @pl.loop(1, n_col)
        def _(i):
            pl.semaphore_signal(barrier, inc=1, device_id={"row": row, "col": (col + i) % n_col},
                                device_id_type=MESH)

        diagonal = ((-1, -1, has_up & has_left), (-1, 1, has_up & has_right),
                    (1, -1, has_down & has_left), (1, 1, has_down & has_right))
        expected = n_row + n_col - 2
        for dr, dc, there in diagonal:
            @pl.when(there)
            def _(dr=dr, dc=dc):
                pl.semaphore_signal(barrier, inc=1, device_id={"row": row + dr, "col": col + dc},
                                    device_id_type=MESH)
            expected = expected + there.astype(jnp.int32)

        @pl.when(jnp.logical_not(has_up))
        def _():
            E[:, 0:T, 0:8, :] = jnp.zeros((3, T, 8, 128), F32)
            L[0:T, 0:8, :] = jnp.zeros((T, 8, 128), jnp.int32)

        @pl.when(jnp.logical_not(has_down))
        def _():
            E[:, 0:T, 136:144, :] = jnp.zeros((3, T, 8, 128), F32)
            L[0:T, 136:144, :] = jnp.zeros((T, 8, 128), jnp.int32)

        for cp in loads:
            cp.wait()

        lane = lax.broadcasted_iota(jnp.int32, (128, 128), 1)
        packed = jnp.zeros((128, 128), F32)
        for k in range(4):
            if k < 3:
                first, last = E[k, 0, 8:136, :], E[k, T - 1, 8:136, :]
            else:
                first, last = L[0, 8:136, :].astype(F32), L[T - 1, 8:136, :].astype(F32)
            both = pltpu.roll(jnp.where(lane < 64, first, last), 8 * k + 4, axis=1)
            packed = jnp.where((lane >= 8 * k) & (lane < 8 * k + 8), both, packed)
        strip[...] = packed.T[0:32, :]

        pl.semaphore_wait(barrier, expected)

        def to(r, c):
            return dict(device_id={"row": r, "col": c}, device_id_type=MESH)

        halo = []

        def exchange(slot, s_ref, d_ref, goes, r, c, comes):
            cp = pltpu.make_async_remote_copy(
                src_ref=s_ref, dst_ref=d_ref, send_sem=halo_send.at[slot],
                recv_sem=halo_recv.at[slot], **to(r, c))

            @pl.when(goes)
            def _():
                cp.start()
            halo.append((cp, goes, comes))

        exchange(0, strip, strip_in.at[0], has_right, row, col + 1, has_left)
        exchange(1, strip, strip_in.at[1], has_left, row, col - 1, has_right)
        exchange(2, E.at[:, pl.ds(0, T), pl.ds(8, 8), :], E.at[:, pl.ds(0, T), pl.ds(136, 8), :],
                 has_up, row - 1, col, has_down)
        exchange(3, E.at[:, pl.ds(0, T), pl.ds(128, 8), :], E.at[:, pl.ds(0, T), pl.ds(0, 8), :],
                 has_down, row + 1, col, has_up)
        exchange(4, L.at[pl.ds(0, T), pl.ds(8, 8), :], L.at[pl.ds(0, T), pl.ds(136, 8), :],
                 has_up, row - 1, col, has_down)
        exchange(5, L.at[pl.ds(0, T), pl.ds(128, 8), :], L.at[pl.ds(0, T), pl.ds(0, 8), :],
                 has_down, row + 1, col, has_up)
        slot = 6
        opposite = (diagonal[3][2], diagonal[2][2], diagonal[1][2], diagonal[0][2])
        for q, (dr, dc, there) in enumerate(diagonal):
            rows = pl.ds(8 if dr < 0 else 128, 8)
            j = 0 if dc < 0 else T - 1
            exchange(slot, E.at[:, j, rows, :], corner_in.at[q], there, row + dr, col + dc,
                     opposite[q])
            exchange(slot + 1, L.at[j, rows, :], corner_lab.at[q], there, row + dr, col + dc,
                     opposite[q])
            slot += 2

        for cp, goes, comes in halo:
            @pl.when(comes)
            def _(cp=cp):
                cp.wait_recv()

        sub32 = lax.broadcasted_iota(jnp.int32, (32, 128), 0) % 8
        merged = jnp.where((sub32 < 4) & has_left, strip_in[0],
                           jnp.where((sub32 >= 4) & has_right, strip_in[1], 0.0))
        beside = jnp.concatenate([merged, jnp.zeros((96, 128), F32)], axis=0).T
        outer = (lane < 4) | (lane >= 124)
        for k in range(4):
            tile = jnp.where(outer, pltpu.roll(beside, 128 - (8 * k + 4), axis=1), 0.0)
            if k < 3:
                E[k, T, 8:136, :] = tile
            else:
                L[T, 8:136, :] = tile.astype(jnp.int32)

        lane8 = lax.broadcasted_iota(jnp.int32, (8, 128), 1)
        sub8 = lax.broadcasted_iota(jnp.int32, (8, 128), 0)
        low4, high4 = lane8 < 4, lane8 >= 124
        for rows, from_left, from_right in ((slice(0, 8), 3, 2), (slice(136, 144), 1, 0)):
            l_ok, r_ok = opposite[from_left], opposite[from_right]
            for k in range(3):
                E[k, T, rows, :] = jnp.where(
                    high4 & l_ok, corner_in[from_left, k],
                    jnp.where(low4 & r_ok, corner_in[from_right, k], 0.0))
            L[T, rows, :] = jnp.where(
                high4 & l_ok, corner_lab[from_left],
                jnp.where(low4 & r_ok, corner_lab[from_right], 0))

        col_ok = (low4 & has_right) | (high4 & has_left)
        first_lane, last_lane = lane8 == 0, lane8 == 127

        def stencil(read, rows, rows_up, rows_down, count):
            c = [read(j, rows) for j in range(T + 1)]
            fwd = [pltpu.roll(v, 1, axis=1) for v in c]
            bwd = [pltpu.roll(v, 127, axis=1) for v in c]
            out = []
            for j in range(count):
                left = jnp.where(first_lane, fwd[j - 1], fwd[j])
                right = jnp.where(last_lane, bwd[(j + 1) % (T + 1)], bwd[j])
                near = (read(j, rows_down) + read(j, rows_up)) + (right + left)
                out.append(4.0 * c[j] - near)
            return c, out

        def row_slices(base):
            return pl.ds(base, 8), pl.ds(base - 1, 8), pl.ds(base + 1, 8)

        def store_field(f, rows, tiles, ok):
            for j, v in enumerate(tiles):
                if j == T:
                    v = jnp.where(col_ok, v, 0.0)
                if ok is not None:
                    v = jnp.where(ok, v, 0.0)
                V[f, j, rows, :] = v

        def right_side(base, ok):
            rows, up, down = row_slices(base)
            labels = [L[j, rows, :] for j in range(T + 1)]
            b = [None] * (T + 1)
            for k in range(3):
                _, a = stencil(lambda j, r, k=k: E[k, j, r, :], rows, up, down, T + 1)
                b = a if k == 0 else [
                    jnp.where(lb == k, v, w) for lb, v, w in zip(labels, a, b)]
            store_field(0, rows, b, ok)

        def apply(f, base, ok, count=T + 1):
            rows, up, down = row_slices(base)
            c, a = stencil(lambda j, r: V[f, j, r, :], rows, up, down, count)
            if f < 2:
                store_field(f + 1, rows, a, ok)
            return c, a

        top_ok = has_up | (sub8 == 7)
        bottom_ok = has_down | (sub8 == 0)
        right_side(1, top_ok)
        right_side(135, bottom_ok)

        @pl.loop(1, 17)
        def _(i):
            right_side(pl.multiple_of(8 * i, 8), None)

        def add_up(products):
            while len(products) > 1:
                products = [a + b for a, b in zip(products[::2], products[1::2])]
            return products[0]

        zero8 = jnp.zeros((8, 128), F32)
        sums = []
        for f in range(3):
            if f < 2:
                apply(f, 1, top_ok)
                apply(f, 135, bottom_ok)

            def body(i, carry, f=f):
                c, a = apply(f, pl.multiple_of(8 * i, 8), None, T + 1 if f < 2 else T)
                same = add_up([c[j] * c[j] for j in range(T)])
                next_ = add_up([c[j] * a[j] for j in range(T)])
                return carry[0] + same, carry[1] + next_
            sums += list(lax.fori_loop(1, 17, body, (zero8, zero8)))

        pairs = [(s, zero8) for s in sums]
        for shift in (4, 2, 1):
            pairs = [dd_add(p, (pltpu.roll(p[0], shift, axis=0), pltpu.roll(p[1], shift, axis=0)))
                     for p in pairs]
        hi, lo = zero8, zero8
        for m, p in enumerate(pairs):
            hi, lo = jnp.where(sub8 == m, p[0], hi), jnp.where(sub8 == m, p[1], lo)
        for shift in (64, 32, 16, 8, 4, 2, 1):
            hi, lo = dd_add((hi, lo), (pltpu.roll(hi, shift, axis=1), pltpu.roll(lo, shift, axis=1)))
        line = jnp.where(lane8 == sub8, hi, 0.0) + jnp.where(lane8 == sub8 + 8, lo, 0.0)
        line = jnp.sum(line, axis=0, keepdims=True)

        lane1 = lax.broadcasted_iota(jnp.int32, (1, 128), 1)

        def total(lines):
            err = []
            while len(lines) > 1:
                both = [two_sum(a, b) for a, b in zip(lines[::2], lines[1::2])]
                lines = [b[0] for b in both]
                err += [b[1] for b in both]
            err = add_up(err + [jnp.zeros((1, 128), F32)])
            low = pltpu.roll(lines[0], 120, axis=1) + err
            h, l = two_sum(lines[0], low)
            return jnp.where(lane1 < 8, h, 0.0) + jnp.where(
                (lane1 >= 8) & (lane1 < 16), pltpu.roll(l, 8, axis=1), 0.0)

        def all_reduce(line, buf, phase, n, me, device):
            msg[phase] = line
            buf[me] = line

            @pl.loop(1, n)
            def _(i):
                peer = (me + i) % n
                pltpu.make_async_remote_copy(
                    src_ref=msg.at[phase], dst_ref=buf.at[me], send_sem=red_send.at[phase],
                    recv_sem=red_recv.at[phase], device_id=device(peer),
                    device_id_type=MESH).start()
            rest = buf.at[pl.ds(0, n - 1)]
            pltpu.make_async_copy(rest, rest, red_recv.at[phase]).wait()
            pltpu.make_async_copy(rest, rest, red_send.at[phase]).wait()
            return total([buf[i] for i in range(n)])

        line = all_reduce(line, red_col, 0, n_col, col, lambda p: {"row": row, "col": p})
        line = all_reduce(line, red_row, 1, n_row, row, lambda p: {"row": p, "col": col})

        pick = lambda m: jnp.sum(jnp.where(lane1 == m, line, 0.0), axis=1, keepdims=True)
        n = [(pick(m), pick(m + 8)) for m in range(6)]
        c0, c1, c2 = (jnp.broadcast_to(c, (8, 128)) for c in krylov_weights(n))

        @pl.loop(0, 16)
        def _(i):
            r = pl.multiple_of(8 * i, 8)
            for j in range(T):
                O[j, pl.ds(r, 8), :] = (
                    c0 * V[0, j, pl.ds(r + 8, 8), :] + c1 * V[1, j, pl.ds(r + 8, 8), :]
                    + c2 * V[2, j, pl.ds(r + 8, 8), :])

        outs = [pltpu.make_async_copy(O.at[j], o_blend.at[:, pl.ds(128 * j, 128)], out_sem.at[j])
                for j in range(T)]
        for cp in outs:
            cp.start()

        for j in range(T // 2):
            rows = [O[2 * j + h, pl.ds(0, 64, stride=2), :] + O[2 * j + h, pl.ds(1, 64, stride=2), :]
                    for h in range(2)]
            FI[j] = pool_lanes(jnp.concatenate(rows, axis=1))
        for j in range(T // 4):
            rows = [FI[2 * j + h, pl.ds(0, 32, stride=2), :] + FI[2 * j + h, pl.ds(1, 32, stride=2), :]
                    for h in range(2)]
            GM[row, j] = pool_lanes(jnp.concatenate(rows, axis=1))

        chip, core = row // 2, row % 2
        partner = 2 * chip + 1 - core

        def block_copy(r, target, sem):
            return pltpu.make_async_remote_copy(
                src_ref=GM.at[r], dst_ref=GM.at[r], send_sem=g_send.at[sem], recv_sem=g_recv.at[r],
                **to(target, col))

        @pl.loop(1, n_chip)
        def _(i):
            block_copy(row, 2 * ((chip + i) % n_chip) + core, i).start()
        block_copy(row, partner, 0).start()

        for j in range(T // 2):
            cp = pltpu.make_async_copy(FI.at[j], o_fine.at[:, pl.ds(128 * j, 128)], out_sem.at[T + j])
            cp.start()
            outs.append(cp)

        @pl.loop(1, n_chip)
        def _(i):
            r = 2 * ((chip + n_chip - i) % n_chip) + core
            block_copy(r, partner, 0).wait_recv()
            block_copy(r, partner, n_chip + i).start()

        @pl.loop(0, n_chip)
        def _(i):
            r = 2 * ((chip + n_chip - i) % n_chip) + 1 - core
            block_copy(r, partner, 0).wait_recv()

        for j in range(T // 4):
            cp = pltpu.make_async_copy(GM.at[:, j], o_mid.at[:, :, pl.ds(128 * j, 128)],
                                       out_sem.at[T + T // 2 + j])
            cp.start()
            outs.append(cp)

        @pl.loop(0, n_row // 8)
        def _(i):
            both = [jnp.concatenate(
                [GM[8 * i + r, h, pl.ds(0, 16, stride=2), :] + GM[8 * i + r, h, pl.ds(1, 16, stride=2), :]
                 for r in range(8)], axis=0) for h in range(2)]
            CO[pl.ds(8 * i, 8)] = pool_lanes(jnp.concatenate(both, axis=1)).reshape(8, 16, 128)
        cp = pltpu.make_async_copy(CO, o_coarse, out_sem.at[T + T // 2 + T // 4])
        cp.start()
        outs.append(cp)

        @pl.loop(0, n_chip)
        def _(i):
            block_copy(row, partner, i).wait_send()

        @pl.loop(1, n_chip)
        def _(i):
            block_copy(row, partner, n_chip + i).wait_send()
        for cp, goes, comes in halo:
            @pl.when(goes)
            def _(cp=cp):
                cp.wait_send()
        for cp in outs:
            cp.wait()

    return kernel


def solution(mesh):
    n_row, n_col = mesh.shape["row"], mesh.shape["col"]

    def step(sources, labels):
        hbm = pl.BlockSpec(memory_space=pl.ANY)
        sem = pltpu.SemaphoreType.DMA
        blended, fine, mid, coarse = pl.pallas_call(
            make_kernel(n_row, n_col),
            out_shape=(
                jax.ShapeDtypeStruct((128, 1024), F32),
                jax.ShapeDtypeStruct((64, 512), F32),
                jax.ShapeDtypeStruct((n_row, 32, 256), F32),
                jax.ShapeDtypeStruct((n_row, 16, 128), F32),
            ),
            in_specs=[hbm, hbm],
            out_specs=(hbm, hbm, hbm, hbm),
            scratch_shapes=[
                pltpu.VMEM((3, T + 1, ROWS, 128), F32),
                pltpu.VMEM((T + 1, ROWS, 128), jnp.int32),
                pltpu.VMEM((3, T + 1, ROWS, 128), F32),
                pltpu.VMEM((T, 128, 128), F32),
                pltpu.VMEM((T // 2, 64, 128), F32),
                pltpu.VMEM((n_row, 2, 32, 128), F32),
                pltpu.VMEM((n_row, 16, 128), F32),
                pltpu.VMEM((32, 128), F32),
                pltpu.VMEM((2, 32, 128), F32),
                pltpu.VMEM((4, 3, 8, 128), F32),
                pltpu.VMEM((4, 8, 128), jnp.int32),
                pltpu.VMEM((2, 1, 128), F32),
                pltpu.VMEM((n_row, 1, 128), F32),
                pltpu.VMEM((n_col, 1, 128), F32),
                sem((2 * T,)),
                sem((14,)),
                sem((14,)),
                sem((2,)),
                sem((2,)),
                sem((n_row,)),
                sem((n_row,)),
                sem((T + T // 2 + T // 4 + 1,)),
            ],
            compiler_params=pltpu.CompilerParams(
                collective_id=0, has_side_effects=True, vmem_limit_bytes=48 * 1024 * 1024),
        )(sources, labels)
        return blended, fine, mid.reshape(-1, 256), coarse.reshape(-1, 128)

    return jax.shard_map(
        step,
        mesh=mesh,
        in_specs=(P(None, "row", "col"), P("row", "col")),
        out_specs=(P("row", "col"), P("row", "col"), P(None, "col"), P(None, "col")),
        check_vma=False,
    )
```

time: 307 us -> 52.2 us (0.17)
  blocking collectives: 146 us -> 0 us
  local copies, waits for them, and re-layouts: 79.2 us -> 5.56 us
  starting transfers between devices: 52.7 us -> 0 us
  Pallas kernels: 0 us -> 45.8 us
  between operations: 11 us -> 0.65 us
  waiting for transfers between devices: 8.59 us -> 0 us
  other arithmetic: 8.45 us -> 0 us
    psum x12 -> x0, blocking collectives: 122 us -> none  [by_axis(): value = lax.psum(value, axis)]
    slice x20 -> x0, local copies, waits for them, and re-layouts: 73.6 us -> none  [the longest x3 18.2 us: average_pool(): values[0::2, 0::2] + values[1::2, 0::2] + values[0::2, 1::2]]
    ppermute x16 -> x0, starting transfers between devices: 52.7 us -> none  [the longest x8 39.9 us: padded_2(): lax.ppermute(last, axis, up)]
    pallas_call x0 -> x1, Pallas kernels: none -> 45.8 us  [step(): pl.pallas_call(make_kernel(n_row, n_col), out_shape=(jax.ShapeDtypeStruct...]
    all_to_all x1 -> x0, blocking collectives: 24.6 us -> none  [from_everyone(): return lax.all_to_all(copies, axis, split_axis=0, concat_axis=0, tiled=True)]
    ppermute x16 -> x0, waiting for transfers between devices: 8.59 us -> none  [the longest x8 5.72 us: padded_2(): lax.ppermute(last, axis, up)]
    unnamed x9 -> x8, local copies, waits for them, and re-layouts: 0.99 us -> 5.56 us
  transfers between devices with their start and end apart: 16 -> 0, of which waited for: 5 -> 0; matrix products, arithmetic and copies ran while one was open for 0% -> 0% of each run, Pallas kernels for 0% -> 0%
where the time goes in v1:
time: 52.2 us; the launch traced here: 52 us
  Pallas kernels  45.8 us (88%)
  local copies, waits for them, and re-layouts  5.56 us (11%)
  between operations  0.65 us (1%)
    pallas_call x1, Pallas kernels, step(): pl.pallas_call(make_kernel(n_row, n_col), out_shape=(jax.ShapeDtypeStruct...  45.8 us
    unnamed x8, local copies, waits for them, and re-layouts  5.56 us

profile of v1, /device:TPU:1, one launch (start us, length us, event | category | flops | bytes accessed | tf_op | source)
XLA Modules:
  0.0 52.0 jit_solution(9155577547762960565)
XLA Ops:
  0.6 0.0 copy-start
  0.6 1.4 %copy-done = f32[3,128,1024]{2,1,0:T(8,128)S(1)} copy-done((f32[3,128,1024]{2,1,0:T(8,128)S(1)}, f32[3,128,1024]{2,1,0:T(8,128)}, u32[]{:S(2)}) %copy-start) | copy-done | bytes 1572888
  2.0 0.0 copy-start.1
  2.0 1.0 %copy-done.1 = s32[128,1024]{1,0:T(8,128)S(1)} copy-done((s32[128,1024]{1,0:T(8,128)S(1)}, s32[128,1024]{1,0:T(8,128)}, u32[]{:S(2)}) %copy-start.1) | copy-done | bytes 524312
  3.1 45.8 %shard_map.57 = (f32[128,1024]{1,0:T(8,128)S(1)}, f32[64,512]{1,0:T(8,128)S(1)}, f32[32,32,256]{2,1,0:T(8,128)S(1)}, f32[32,16,128]{2,1,0:T(8,128)S(1)}) custom-call(f32[3,128,1024]{2,1,0:T(8,128)S(1)} %copy-done, s32[128,1024]{1,0:T(8,128)S(1)} %copy-done.1), custom_call_target="tpu_custom_call" | custom-call | tf_op jit(solution)/shard_map/pallas_call | solution.py:436
  48.9 0.8 %copy.10 = f32[128,1024]{1,0:T(8,128)} copy(f32[128,1024]{1,0:T(8,128)S(1)} %get-tuple-element.16) | data formatting | bytes 1048576
  49.7 0.7 %copy.11 = f32[64,512]{1,0:T(8,128)} copy(f32[64,512]{1,0:T(8,128)S(1)} %get-tuple-element.17) | data formatting | bytes 262144
  50.4 1.0 %copy.12 = f32[1024,256]{1,0:T(8,128)} copy(f32[1024,256]{1,0:T(8,128)S(1)} %bitcast.2) | data formatting | bytes 2097152
  51.3 0.7 %copy.13 = f32[512,128]{1,0:T(8,128)} copy(f32[512,128]{1,0:T(8,128)S(1)} %bitcast.3) | data formatting | bytes 524288
Async XLA Ops:
  0.6 1.4 %copy-start = (f32[3,128,1024]{2,1,0:T(8,128)S(1)}, f32[3,128,1024]{2,1,0:T(8,128)}, u32[]{:S(2)}) copy-start(f32[3,128,1024]{2,1,0:T(8,128)} %src.1) | copy-start | bytes 4718596
  2.0 1.0 %copy-start.1 = (s32[128,1024]{1,0:T(8,128)S(1)}, s32[128,1024]{1,0:T(8,128)}, u32[]{:S(2)}) copy-start(s32[128,1024]{1,0:T(8,128)} %lab.1) | copy-start | bytes 1572868

commit v2 on v1

--- a/solution.py
+++ b/solution.py
@@ -9,7 +9,8 @@
 F32 = jnp.float32
 T = 8
 ROWS = 144
-LANE_ROLL = 127
+X = 4
+UNROLL = 4
 
 
 def two_sum(a, b):
@@ -74,33 +75,36 @@
     return c0[0], c1[0], c2[0]
 
 
-def pool_lanes(pair):
-    src = lax.broadcasted_iota(jnp.int32, (256, 128), 0)
-    dst = lax.broadcasted_iota(jnp.int32, (256, 128), 1)
-    weight = jnp.where(src // 2 == dst, 0.25, 0.0).astype(jnp.bfloat16)
-    hi = pair.astype(jnp.bfloat16)
-    rest = pair - hi.astype(F32)
+def weights(k, step, value, shift=0):
+    src = lax.broadcasted_iota(jnp.int32, (k, 128), 0)
+    dst = lax.broadcasted_iota(jnp.int32, (k, 128), 1)
+    return jnp.where(src // step + shift == dst, value, 0.0).astype(jnp.bfloat16)
+
+
+def exact_dot(v, weight):
+    hi = v.astype(jnp.bfloat16)
+    rest = v - hi.astype(F32)
     mid = rest.astype(jnp.bfloat16)
     low = (rest - mid.astype(F32)).astype(jnp.bfloat16)
-    dot = lambda v: jnp.dot(v, weight, preferred_element_type=F32)
+    dot = lambda p: jnp.dot(p, weight, preferred_element_type=F32)
     return dot(hi) + dot(mid) + dot(low)
 
 
 def make_kernel(n_row, n_col):
-    n_chip = n_row // 2
-
-    def kernel(src, lab, o_blend, o_fine, o_mid, o_coarse,
-               E, L, V, O, FI, GM, CO, strip, strip_in, corner_in, corner_lab,
+    n_y = n_row // (2 * X)
+
+    def kernel(src, lab, O, FI, H, CO,
+               E, L, V, MB, PB, FB, strip, strip_in, corner_in, corner_lab,
                msg, red_row, red_col,
                load_sem, halo_send, halo_recv, red_send, red_recv,
-               g_send, g_recv, out_sem):
+               p_send, p_recv, h_send, h_recv):
         row = lax.axis_index("row")
         col = lax.axis_index("col")
         has_up, has_down = row > 0, row < n_row - 1
         has_left, has_right = col > 0, col < n_col - 1
 
         loads = []
-        for j in range(T):
+        for j in (0, T - 1, *range(1, T - 1)):
             lanes = pl.ds(128 * j, 128)
             loads.append(pltpu.make_async_copy(
                 src.at[:, :, lanes], E.at[:, j, pl.ds(8, 128), :], load_sem.at[2 * j]))
@@ -141,7 +145,7 @@
             E[:, 0:T, 136:144, :] = jnp.zeros((3, T, 8, 128), F32)
             L[0:T, 136:144, :] = jnp.zeros((T, 8, 128), jnp.int32)
 
-        for cp in loads:
+        for cp in loads[:4]:
             cp.wait()
 
         lane = lax.broadcasted_iota(jnp.int32, (128, 128), 1)
@@ -155,6 +159,8 @@
             packed = jnp.where((lane >= 8 * k) & (lane < 8 * k + 8), both, packed)
         strip[...] = packed.T[0:32, :]
 
+        for cp in loads[4:]:
+            cp.wait()
         pl.semaphore_wait(barrier, expected)
 
         def to(r, c):
@@ -271,9 +277,10 @@
         right_side(1, top_ok)
         right_side(135, bottom_ok)
 
-        @pl.loop(1, 17)
-        def _(i):
+        def body(i, carry):
             right_side(pl.multiple_of(8 * i, 8), None)
+            return carry
+        lax.fori_loop(1, 17, body, 0, unroll=UNROLL)
 
         def add_up(products):
             while len(products) > 1:
@@ -292,7 +299,7 @@
                 same = add_up([c[j] * c[j] for j in range(T)])
                 next_ = add_up([c[j] * a[j] for j in range(T)])
                 return carry[0] + same, carry[1] + next_
-            sums += list(lax.fori_loop(1, 17, body, (zero8, zero8)))
+            sums += list(lax.fori_loop(1, 17, body, (zero8, zero8), unroll=UNROLL))
 
         pairs = [(s, zero8) for s in sums]
         for shift in (4, 2, 1):
@@ -320,137 +327,187 @@
             return jnp.where(lane1 < 8, h, 0.0) + jnp.where(
                 (lane1 >= 8) & (lane1 < 16), pltpu.roll(l, 8, axis=1), 0.0)
 
-        def all_reduce(line, buf, phase, n, me, device):
+        def reduce_start(line, buf, phase, n, me, device):
             msg[phase] = line
             buf[me] = line
 
             @pl.loop(1, n)
             def _(i):
-                peer = (me + i) % n
                 pltpu.make_async_remote_copy(
                     src_ref=msg.at[phase], dst_ref=buf.at[me], send_sem=red_send.at[phase],
-                    recv_sem=red_recv.at[phase], device_id=device(peer),
+                    recv_sem=red_recv.at[phase], device_id=device((me + i) % n),
                     device_id_type=MESH).start()
+
+        def reduce_end(buf, phase, n):
             rest = buf.at[pl.ds(0, n - 1)]
             pltpu.make_async_copy(rest, rest, red_recv.at[phase]).wait()
+            return total([buf[i] for i in range(n)])
+
+        def reduce_sent(buf, phase, n):
+            rest = buf.at[pl.ds(0, n - 1)]
             pltpu.make_async_copy(rest, rest, red_send.at[phase]).wait()
-            return total([buf[i] for i in range(n)])
-
-        line = all_reduce(line, red_col, 0, n_col, col, lambda p: {"row": row, "col": p})
-        line = all_reduce(line, red_row, 1, n_row, row, lambda p: {"row": p, "col": col})
+
+        reduce_start(line, red_col, 0, n_col, col, lambda p: {"row": row, "col": p})
+
+        core, x, y = row % 2, (row // 2) % X, row // (2 * X)
+        w4 = weights(512, 4, 1 / 16)
+        for h in range(2):
+            quads = jnp.concatenate([
+                jnp.concatenate([
+                    (V[k, 4 * h + j, pl.ds(8, 32, stride=4), :] + V[k, 4 * h + j, pl.ds(9, 32, stride=4), :])
+                    + (V[k, 4 * h + j, pl.ds(10, 32, stride=4), :] + V[k, 4 * h + j, pl.ds(11, 32, stride=4), :])
+                    for j in range(4)], axis=1) for k in range(3)], axis=0)
+            MB[h] = exact_dot(quads, w4).reshape(3, 32, 128)
+
+        def early(h, slot, peer, sem):
+            return pltpu.make_async_remote_copy(
+                src_ref=MB.at[h], dst_ref=PB.at[slot], send_sem=p_send.at[sem],
+                recv_sem=p_recv.at[slot], **to(peer, col))
+
+        early(1 - core, 2 * jnp.where(core == 0, y, x) + core, row + 1 - 2 * core, 0).start()
+        for i in range(1, X):
+            early(0, 2 * x + core, (y * X + (x + i) % X) * 2, i).start()
+        for i in range(1, n_y):
+            early(1, 2 * y + core, (((y + i) % n_y) * X + x) * 2 + 1, X - 1 + i).start()
+        own_slot = 2 * jnp.where(core == 0, x, y) + core
+        PB[own_slot] = MB[core]
+
+        w2 = weights(256, 2, 0.25)
+        def fine_part(j):
+            pairs2 = jnp.concatenate([
+                jnp.concatenate([V[k, 2 * j + h, pl.ds(8, 64, stride=2), :]
+                                 + V[k, 2 * j + h, pl.ds(9, 64, stride=2), :] for h in range(2)], axis=1)
+                for k in range(3)], axis=0)
+            FB[j] = exact_dot(pairs2, w2).reshape(3, 64, 128)
+
+        fine_part(0)
+        fine_part(1)
+        line = reduce_end(red_col, 0, n_col)
+        reduce_start(line, red_row, 1, n_row, row, lambda p: {"row": p, "col": col})
+        fine_part(2)
+        fine_part(3)
+        CO[...] = jnp.zeros((n_y, X, 2, 16, 128), F32)
+        reduce_sent(red_col, 0, n_col)
+
+        def early_here(i):
+            slot = lax.rem(own_slot + i, 8)
+            early(0, slot, row, 0).wait_recv()
+
+        for i in range(1, 8):
+            early_here(i)
+        line = reduce_end(red_row, 1, n_row)
 
         pick = lambda m: jnp.sum(jnp.where(lane1 == m, line, 0.0), axis=1, keepdims=True)
         n = [(pick(m), pick(m + 8)) for m in range(6)]
         c0, c1, c2 = (jnp.broadcast_to(c, (8, 128)) for c in krylov_weights(n))
 
-        @pl.loop(0, 16)
-        def _(i):
+        mine = jnp.where(core == 0, y, x)
+        for slot in range(8):
+            for r in range(4):
+                rows = pl.ds(8 * r, 8)
+                H[core, mine, slot // 2, slot % 2, rows, :] = (
+                    c0 * PB[slot, 0, rows, :] + c1 * PB[slot, 1, rows, :] + c2 * PB[slot, 2, rows, :])
+
+        def late(h, q, peer, sem):
+            return pltpu.make_async_remote_copy(
+                src_ref=H.at[h, q], dst_ref=H.at[h, q], send_sem=h_send.at[sem],
+                recv_sem=h_recv.at[h, q], **to(peer, col))
+
+        partner = row + 1 - 2 * core
+        for i in (2, 1, 3):
+            peer = jnp.where(core == 0, (((y + i) % n_y) * X + x) * 2, (y * X + (x + i) % X) * 2 + 1)
+            late(core, mine, peer, i).start()
+        late(core, mine, partner, 0).start()
+
+        def body(i, carry):
             r = pl.multiple_of(8 * i, 8)
             for j in range(T):
                 O[j, pl.ds(r, 8), :] = (
                     c0 * V[0, j, pl.ds(r + 8, 8), :] + c1 * V[1, j, pl.ds(r + 8, 8), :]
                     + c2 * V[2, j, pl.ds(r + 8, 8), :])
-
-        outs = [pltpu.make_async_copy(O.at[j], o_blend.at[:, pl.ds(128 * j, 128)], out_sem.at[j])
-                for j in range(T)]
-        for cp in outs:
-            cp.start()
-
-        for j in range(T // 2):
-            rows = [O[2 * j + h, pl.ds(0, 64, stride=2), :] + O[2 * j + h, pl.ds(1, 64, stride=2), :]
-                    for h in range(2)]
-            FI[j] = pool_lanes(jnp.concatenate(rows, axis=1))
-        for j in range(T // 4):
-            rows = [FI[2 * j + h, pl.ds(0, 32, stride=2), :] + FI[2 * j + h, pl.ds(1, 32, stride=2), :]
-                    for h in range(2)]
-            GM[row, j] = pool_lanes(jnp.concatenate(rows, axis=1))
-
-        chip, core = row // 2, row % 2
-        partner = 2 * chip + 1 - core
-
-        def block_copy(r, target, sem):
-            return pltpu.make_async_remote_copy(
-                src_ref=GM.at[r], dst_ref=GM.at[r], send_sem=g_send.at[sem], recv_sem=g_recv.at[r],
-                **to(target, col))
-
-        @pl.loop(1, n_chip)
-        def _(i):
-            block_copy(row, 2 * ((chip + i) % n_chip) + core, i).start()
-        block_copy(row, partner, 0).start()
-
-        for j in range(T // 2):
-            cp = pltpu.make_async_copy(FI.at[j], o_fine.at[:, pl.ds(128 * j, 128)], out_sem.at[T + j])
-            cp.start()
-            outs.append(cp)
-
-        @pl.loop(1, n_chip)
-        def _(i):
-            r = 2 * ((chip + n_chip - i) % n_chip) + core
-            block_copy(r, partner, 0).wait_recv()
-            block_copy(r, partner, n_chip + i).start()
-
-        @pl.loop(0, n_chip)
-        def _(i):
-            r = 2 * ((chip + n_chip - i) % n_chip) + 1 - core
-            block_copy(r, partner, 0).wait_recv()
-
-        for j in range(T // 4):
-            cp = pltpu.make_async_copy(GM.at[:, j], o_mid.at[:, :, pl.ds(128 * j, 128)],
-                                       out_sem.at[T + T // 2 + j])
-            cp.start()
-            outs.append(cp)
-
-        @pl.loop(0, n_row // 8)
-        def _(i):
-            both = [jnp.concatenate(
-                [GM[8 * i + r, h, pl.ds(0, 16, stride=2), :] + GM[8 * i + r, h, pl.ds(1, 16, stride=2), :]
-                 for r in range(8)], axis=0) for h in range(2)]
-            CO[pl.ds(8 * i, 8)] = pool_lanes(jnp.concatenate(both, axis=1)).reshape(8, 16, 128)
-        cp = pltpu.make_async_copy(CO, o_coarse, out_sem.at[T + T // 2 + T // 4])
-        cp.start()
-        outs.append(cp)
-
-        @pl.loop(0, n_chip)
-        def _(i):
-            block_copy(row, partner, i).wait_send()
-
-        @pl.loop(1, n_chip)
-        def _(i):
-            block_copy(row, partner, n_chip + i).wait_send()
+            return carry
+        lax.fori_loop(0, 16, body, 0, unroll=2)
+
+        def body(i, carry):
+            rows = pl.ds(pl.multiple_of(8 * i, 8), 8)
+            for j in range(T // 2):
+                FI[j, rows, :] = (
+                    c0 * FB[j, 0, rows, :] + c1 * FB[j, 1, rows, :] + c2 * FB[j, 2, rows, :])
+            return carry
+        lax.fori_loop(0, 8, body, 0, unroll=2)
+
+        def coarse(h, q):
+            rows = [H[h, q, s // 2, s % 2, pl.ds(0, 16, stride=2), :]
+                    + H[h, q, s // 2, s % 2, pl.ds(1, 16, stride=2), :] for s in range(8)]
+            out = exact_dot(jnp.concatenate(rows, axis=0), weights(128, 2, 0.25, 64 * h))
+            for s in range(8):
+                at = (jnp.where(h == 0, q, s // 2), jnp.where(h == 0, s // 2, q), s % 2)
+                CO[at] = CO[at] + out[16 * s:16 * s + 16, :]
+
+        coarse(core, mine)
+        for i in (1, 3, 2):
+            q = (mine + i) % X
+            late(core, q, partner, 0).wait_recv()
+            late(core, q, partner, X - 1 + i).start()
+            coarse(core, q)
+        other = 1 - core
+        for i in (0, 1, 3, 2):
+            q = (jnp.where(core == 0, x, y) + i) % X
+            late(other, q, partner, 0).wait_recv()
+            coarse(other, q)
+
+        for i in range(7):
+            early(0, 0, row, i).wait_send()
+        for i in range(7):
+            late(0, 0, row, i).wait_send()
+        reduce_sent(red_row, 1, n_row)
         for cp, goes, comes in halo:
             @pl.when(goes)
             def _(cp=cp):
                 cp.wait_send()
-        for cp in outs:
-            cp.wait()
 
     return kernel
+
+
+def write_out(O, FI, H, CO, o_blend, o_fine, o_mid, o_coarse, sem):
+    copies = [(H.at[0], o_mid.at[:, :, :, :, pl.ds(0, 128)])]
+    copies += [(H.at[1, q], o_mid.at[:, q, :, :, pl.ds(128, 128)]) for q in range(X)]
+    copies += [(O.at[j], o_blend.at[:, pl.ds(128 * j, 128)]) for j in range(T)]
+    copies += [(CO, o_coarse)]
+    copies += [(FI.at[j], o_fine.at[:, pl.ds(128 * j, 128)]) for j in range(T // 2)]
+    copies = [pltpu.make_async_copy(a, b, sem.at[i]) for i, (a, b) in enumerate(copies)]
+    for cp in copies:
+        cp.start()
+    for cp in copies:
+        cp.wait()
 
 
 def solution(mesh):
     n_row, n_col = mesh.shape["row"], mesh.shape["col"]
 
+    n_y = n_row // (2 * X)
+
     def step(sources, labels):
-        hbm = pl.BlockSpec(memory_space=pl.ANY)
+        hbm = pl.BlockSpec(memory_space=pltpu.HBM)
+        vmem = pl.BlockSpec(memory_space=pltpu.VMEM)
         sem = pltpu.SemaphoreType.DMA
-        blended, fine, mid, coarse = pl.pallas_call(
+        parts = pl.pallas_call(
             make_kernel(n_row, n_col),
             out_shape=(
-                jax.ShapeDtypeStruct((128, 1024), F32),
-                jax.ShapeDtypeStruct((64, 512), F32),
-                jax.ShapeDtypeStruct((n_row, 32, 256), F32),
-                jax.ShapeDtypeStruct((n_row, 16, 128), F32),
+                jax.ShapeDtypeStruct((T, 128, 128), F32),
+                jax.ShapeDtypeStruct((T // 2, 64, 128), F32),
+                jax.ShapeDtypeStruct((2, 4, 4, 2, 32, 128), F32),
+                jax.ShapeDtypeStruct((n_y, X, 2, 16, 128), F32),
             ),
             in_specs=[hbm, hbm],
-            out_specs=(hbm, hbm, hbm, hbm),
+            out_specs=(vmem, vmem, vmem, vmem),
             scratch_shapes=[
                 pltpu.VMEM((3, T + 1, ROWS, 128), F32),
                 pltpu.VMEM((T + 1, ROWS, 128), jnp.int32),
                 pltpu.VMEM((3, T + 1, ROWS, 128), F32),
-                pltpu.VMEM((T, 128, 128), F32),
-                pltpu.VMEM((T // 2, 64, 128), F32),
-                pltpu.VMEM((n_row, 2, 32, 128), F32),
-                pltpu.VMEM((n_row, 16, 128), F32),
+                pltpu.VMEM((2, 3, 32, 128), F32),
+                pltpu.VMEM((8, 3, 32, 128), F32),
+                pltpu.VMEM((T // 2, 3, 64, 128), F32),
                 pltpu.VMEM((32, 128), F32),
                 pltpu.VMEM((2, 32, 128), F32),
                 pltpu.VMEM((4, 3, 8, 128), F32),
@@ -463,13 +520,27 @@
                 sem((14,)),
                 sem((2,)),
                 sem((2,)),
-                sem((n_row,)),
-                sem((n_row,)),
-                sem((T + T // 2 + T // 4 + 1,)),
+                sem((7,)),
+                sem((8,)),
+                sem((7,)),
+                sem((2, 4)),
             ],
             compiler_params=pltpu.CompilerParams(
-                collective_id=0, has_side_effects=True, vmem_limit_bytes=48 * 1024 * 1024),
-        )(sources, labels)
+                collective_id=0, has_side_effects=True, vmem_limit_bytes=40 * 1024 * 1024),
+        )(pltpu.with_memory_space_constraint(sources, pltpu.HBM), pltpu.with_memory_space_constraint(labels, pltpu.HBM))
+        blended, fine, mid, coarse = pl.pallas_call(
+            write_out,
+            out_shape=(
+                jax.ShapeDtypeStruct((128, 1024), F32),
+                jax.ShapeDtypeStruct((64, 512), F32),
+                jax.ShapeDtypeStruct((n_y, X, 2, 32, 256), F32),
+                jax.ShapeDtypeStruct((n_y, X, 2, 16, 128), F32),
+            ),
+            in_specs=[vmem] * 4,
+            out_specs=(hbm,) * 4,
+            scratch_shapes=[sem((5 + T + 1 + T // 2,))],
+            compiler_params=pltpu.CompilerParams(vmem_limit_bytes=1024 * 1024),
+        )(*parts)
         return blended, fine, mid.reshape(-1, 256), coarse.reshape(-1, 128)
 
     return jax.shard_map(

time: 52.2 us -> 39.4 us (0.75)
  Pallas kernels: 45.8 us -> 38.7 us
  local copies, waits for them, and re-layouts: 5.56 us -> 0 us
    pallas_call x1, Pallas kernels: 45.8 us -> 37.3 us  [step(): pl.pallas_call(make_kernel(n_row, n_col), out_shape=(jax.ShapeDtypeStruct...]
    unnamed x8 -> x0, local copies, waits for them, and re-layouts: 5.56 us -> none
    pallas_call x0 -> x1, Pallas kernels: none -> 1.41 us  [step(): pl.pallas_call(write_out, out_shape=(jax.ShapeDtypeStruct((128, 1024), F3...]
where the time goes in v2:
time: 39.4 us; the launch traced here: 39.3 us
  Pallas kernels  38.7 us (98%)
  between operations  0.64 us (2%)
    pallas_call x1, Pallas kernels, step(): pl.pallas_call(make_kernel(n_row, n_col), out_shape=(jax.ShapeDtypeStruct...  37.3 us
    pallas_call x1, Pallas kernels, step(): pl.pallas_call(write_out, out_shape=(jax.ShapeDtypeStruct((128, 1024), F3...  1.41 us

profile of v2, /device:TPU:1, one launch (start us, length us, event | category | flops | bytes accessed | tf_op | source)
XLA Modules:
  0.0 39.3 jit_solution(15225676237035109426)
XLA Ops:
  0.6 37.3 %shard_map.57 = (f32[8,128,128]{2,1,0:T(8,128)S(1)}, f32[4,64,128]{2,1,0:T(8,128)S(1)}, f32[2,4,4,2,32,128]{5,4,3,2,1,0:T(8,128)S(1)}, f32[4,4,2,16,128]{4,3,2,1,0:T(8,128)S(1)}) custom-call(f32[3,128,1024]{2,1,0:T(8,128)} %src.1, s32[128,1024]{1,0:T(8,128)} %lab.1), custom_call_target="tpu_custom_call" | custom-call | tf_op jit(solution)/shard_map/pallas_call | solution.py:494
  37.9 1.4 %shard_map.58 = (f32[128,1024]{1,0:T(8,128)}, f32[64,512]{1,0:T(8,128)}, f32[4,4,2,32,256]{4,3,2,1,0:T(8,128)}, f32[4,4,2,16,128]{4,3,2,1,0:T(8,128)}) custom-call(f32[8,128,128]{2,1,0:T(8,128)S(1)} %get-tuple-element.12.O, f32[4,64,128]{2,1,0:T(8,128)S(1)} %get-tuple-element.13.FI, f32[2,4,4,2,32,128]{5,4,3,2,1,0:T(8,128)S(1)} %get-tuple-element.14.H, ...), custom_call_target="tpu_custom_call" | custom-call | tf_op jit(solution)/shard_map/pallas_call | solution.py:531

commit v3 on v2

--- a/solution.py
+++ b/solution.py
@@ -10,7 +10,9 @@
 T = 8
 ROWS = 144
 X = 4
-UNROLL = 4
+UNROLL = 16
+UNROLL_B = 4
+UNROLL_C = 8
 
 
 def two_sum(a, b):
@@ -94,10 +96,10 @@
     n_y = n_row // (2 * X)
 
     def kernel(src, lab, O, FI, H, CO,
-               E, L, V, MB, PB, FB, strip, strip_in, corner_in, corner_lab,
+               E, L, V, XE, RU, RD, LU, LD, MB, PB, FB, strip, strip_in, corner_in, corner_lab,
                msg, red_row, red_col,
                load_sem, halo_send, halo_recv, red_send, red_recv,
-               p_send, p_recv, h_send, h_recv):
+               p_send, p_recv, h_send, h_recv, known):
         row = lax.axis_index("row")
         col = lax.axis_index("col")
         has_up, has_down = row > 0, row < n_row - 1
@@ -113,37 +115,37 @@
         for cp in loads:
             cp.start()
 
+        core, x, y = row % 2, (row // 2) % X, row // (2 * X)
+
+        def at(dx=0, dy=0, dcore=0, dcol=0):
+            r = (((y + dy) % n_y) * X + (x + dx) % X) * 2 + (core + dcore) % 2
+            return {"row": r, "col": (col + dcol) % n_col}
+
+        def signal(sem, device):
+            pl.semaphore_signal(sem, inc=1, device_id=device, device_id_type=MESH)
+
         barrier = pltpu.get_barrier_semaphore()
-
-        @pl.loop(1, n_row)
-        def _(i):
-            pl.semaphore_signal(barrier, inc=1, device_id={"row": (row + i) % n_row, "col": col},
-                                device_id_type=MESH)
-
-        @pl.loop(1, n_col)
-        def _(i):
-            pl.semaphore_signal(barrier, inc=1, device_id={"row": row, "col": (col + i) % n_col},
-                                device_id_type=MESH)
-
+        beside_us = [at(dcore=1), at(dx=1), at(dx=-1), at(dy=1), at(dy=-1), at(dcol=1), at(dcol=-1)]
+        for device in beside_us:
+            signal(barrier, device)
+        step = 2 * core - 1
+        cross = jnp.where(core == 1, has_down, has_up)
         diagonal = ((-1, -1, has_up & has_left), (-1, 1, has_up & has_right),
                     (1, -1, has_down & has_left), (1, 1, has_down & has_right))
-        expected = n_row + n_col - 2
+        expected = len(beside_us) + cross.astype(jnp.int32)
+
+        @pl.when(cross)
+        def _():
+            signal(barrier, {"row": row + step, "col": col})
         for dr, dc, there in diagonal:
             @pl.when(there)
             def _(dr=dr, dc=dc):
-                pl.semaphore_signal(barrier, inc=1, device_id={"row": row + dr, "col": col + dc},
-                                    device_id_type=MESH)
+                signal(barrier, {"row": row + dr, "col": col + dc})
             expected = expected + there.astype(jnp.int32)
 
-        @pl.when(jnp.logical_not(has_up))
-        def _():
-            E[:, 0:T, 0:8, :] = jnp.zeros((3, T, 8, 128), F32)
-            L[0:T, 0:8, :] = jnp.zeros((T, 8, 128), jnp.int32)
-
-        @pl.when(jnp.logical_not(has_down))
-        def _():
-            E[:, 0:T, 136:144, :] = jnp.zeros((3, T, 8, 128), F32)
-            L[0:T, 136:144, :] = jnp.zeros((T, 8, 128), jnp.int32)
+        for rows in (slice(0, 8), slice(136, 144)):
+            E[:, 0:T, rows, :] = jnp.zeros((3, T, 8, 128), F32)
+            L[0:T, rows, :] = jnp.zeros((T, 8, 128), jnp.int32)
 
         for cp in loads[:4]:
             cp.wait()
@@ -180,13 +182,14 @@
 
         exchange(0, strip, strip_in.at[0], has_right, row, col + 1, has_left)
         exchange(1, strip, strip_in.at[1], has_left, row, col - 1, has_right)
-        exchange(2, E.at[:, pl.ds(0, T), pl.ds(8, 8), :], E.at[:, pl.ds(0, T), pl.ds(136, 8), :],
+        first4, last4 = pl.ds(8, 4), pl.ds(132, 4)
+        exchange(2, E.at[:, pl.ds(0, T), first4, :], RD.at[:, :, pl.ds(0, 4), :],
                  has_up, row - 1, col, has_down)
-        exchange(3, E.at[:, pl.ds(0, T), pl.ds(128, 8), :], E.at[:, pl.ds(0, T), pl.ds(0, 8), :],
+        exchange(3, E.at[:, pl.ds(0, T), last4, :], RU.at[:, :, pl.ds(4, 4), :],
                  has_down, row + 1, col, has_up)
-        exchange(4, L.at[pl.ds(0, T), pl.ds(8, 8), :], L.at[pl.ds(0, T), pl.ds(136, 8), :],
+        exchange(4, L.at[pl.ds(0, T), first4, :], LD.at[:, pl.ds(0, 4), :],
                  has_up, row - 1, col, has_down)
-        exchange(5, L.at[pl.ds(0, T), pl.ds(128, 8), :], L.at[pl.ds(0, T), pl.ds(0, 8), :],
+        exchange(5, L.at[pl.ds(0, T), last4, :], LU.at[:, pl.ds(4, 4), :],
                  has_down, row + 1, col, has_up)
         slot = 6
         opposite = (diagonal[3][2], diagonal[2][2], diagonal[1][2], diagonal[0][2])
@@ -199,6 +202,102 @@
                      opposite[q])
             slot += 2
 
+        lane8 = lax.broadcasted_iota(jnp.int32, (8, 128), 1)
+        sub8 = lax.broadcasted_iota(jnp.int32, (8, 128), 0)
+        low4, high4 = lane8 < 4, lane8 >= 124
+        col_ok = (low4 & has_right) | (high4 & has_left)
+        first_lane, last_lane = lane8 == 0, lane8 == 127
+
+        def stencil(read, rows, rows_up, rows_down, count):
+            c = [read(j, rows) for j in range(T + 1)]
+            fwd = [pltpu.roll(v, 1, axis=1) for v in c]
+            bwd = [pltpu.roll(v, 127, axis=1) for v in c]
+            out = []
+            for j in range(count):
+                left = jnp.where(first_lane, fwd[j - 1], fwd[j])
+                right = jnp.where(last_lane, bwd[(j + 1) % (T + 1)], bwd[j])
+                near = (read(j, rows_down) + read(j, rows_up)) + (right + left)
+                out.append(4.0 * c[j] - near)
+            return c, out
+
+        def row_slices(base):
+            return pl.ds(base, 8), pl.ds(base - 1, 8), pl.ds(base + 1, 8)
+
+        def store_field(f, rows, tiles, ok):
+            for j, v in enumerate(tiles):
+                if j == T:
+                    v = jnp.where(col_ok, v, 0.0)
+                if ok is not None:
+                    v = jnp.where(ok, v, 0.0)
+                V[f, j, rows, :] = v
+
+        def right_side(base, ok):
+            rows, up, down = row_slices(base)
+            labels = [L[j, rows, :] for j in range(T + 1)]
+            b = [None] * (T + 1)
+            for k in range(3):
+                _, a = stencil(lambda j, r, k=k: E[k, j, r, :], rows, up, down, T + 1)
+                b = a if k == 0 else [
+                    jnp.where(lb == k, v, w) for lb, v, w in zip(labels, a, b)]
+            store_field(0, rows, b, ok)
+
+        def apply(f, base, ok, count=T + 1):
+            rows, up, down = row_slices(base)
+            c, a = stencil(lambda j, r: V[f, j, r, :], rows, up, down, count)
+            if f < 2:
+                store_field(f + 1, rows, a, ok)
+            return c, a
+
+        def choose(labels, values):
+            return jnp.where(labels == 0, values[0], jnp.where(labels == 1, values[1], values[2]))
+
+        def right_side_alone(base):
+            rows, up, down = row_slices(base)
+            labels = [L[j, rows, :] for j in range(T)]
+            b = None
+            for k in range(3):
+                c = [E[k, j, rows, :] for j in range(T)]
+                fwd = [pltpu.roll(v, 1, axis=1) for v in c]
+                bwd = [pltpu.roll(v, 127, axis=1) for v in c]
+                XE[k, rows, :] = jnp.where(first_lane, fwd[T - 1], bwd[0])
+                a = []
+                for j in range(T):
+                    left = jnp.where(first_lane, fwd[j - 1] if j else 0.0, fwd[j])
+                    right = jnp.where(last_lane, bwd[j + 1] if j < T - 1 else 0.0, bwd[j])
+                    near = (E[k, j, down, :] + E[k, j, up, :]) + (right + left)
+                    a.append(4.0 * c[j] - near)
+                b = a if k == 0 else [jnp.where(lb == k, v, w) for lb, v, w in zip(labels, a, b)]
+            for j in range(T):
+                V[0, j, rows, :] = b[j]
+
+        def right_side_beside(base):
+            rows, up, down = row_slices(base)
+            fwd = [pltpu.roll(E[k, T, rows, :], 1, axis=1) for k in range(3)]
+            bwd = [pltpu.roll(E[k, T, rows, :], 127, axis=1) for k in range(3)]
+            a = []
+            for k in range(3):
+                left = jnp.where(first_lane, XE[k, rows, :], fwd[k])
+                right = jnp.where(last_lane, XE[k, rows, :], bwd[k])
+                near = (E[k, T, down, :] + E[k, T, up, :]) + (right + left)
+                a.append(4.0 * E[k, T, rows, :] - near)
+            V[0, T, rows, :] = jnp.where(col_ok, choose(L[T, rows, :], a), 0.0)
+            V[0, 0, rows, :] = V[0, 0, rows, :] - jnp.where(first_lane, choose(L[0, rows, :], fwd), 0.0)
+            V[0, T - 1, rows, :] = V[0, T - 1, rows, :] - jnp.where(
+                last_lane, choose(L[T - 1, rows, :], bwd), 0.0)
+
+        for device in beside_us:
+            signal(known.at[0], device)
+
+        def body(i, carry):
+            right_side_alone(pl.multiple_of(8 * i, 8))
+            return carry
+        lax.fori_loop(1, 17, body, 0, unroll=UNROLL_B)
+
+        pl.semaphore_wait(known.at[0], len(beside_us))
+        two_away = [at(dx=2), at(dy=2), at(dcol=2), at(dcol=-2)]
+        for device in two_away:
+            signal(known.at[1], device)
+
         for cp, goes, comes in halo:
             @pl.when(comes)
             def _(cp=cp):
@@ -216,9 +315,6 @@
             else:
                 L[T, 8:136, :] = tile.astype(jnp.int32)
 
-        lane8 = lax.broadcasted_iota(jnp.int32, (8, 128), 1)
-        sub8 = lax.broadcasted_iota(jnp.int32, (8, 128), 0)
-        low4, high4 = lane8 < 4, lane8 >= 124
         for rows, from_left, from_right in ((slice(0, 8), 3, 2), (slice(136, 144), 1, 0)):
             l_ok, r_ok = opposite[from_left], opposite[from_right]
             for k in range(3):
@@ -229,58 +325,33 @@
                 high4 & l_ok, corner_lab[from_left],
                 jnp.where(low4 & r_ok, corner_lab[from_right], 0))
 
-        col_ok = (low4 & has_right) | (high4 & has_left)
-        first_lane, last_lane = lane8 == 0, lane8 == 127
-
-        def stencil(read, rows, rows_up, rows_down, count):
-            c = [read(j, rows) for j in range(T + 1)]
-            fwd = [pltpu.roll(v, 1, axis=1) for v in c]
-            bwd = [pltpu.roll(v, 127, axis=1) for v in c]
-            out = []
-            for j in range(count):
-                left = jnp.where(first_lane, fwd[j - 1], fwd[j])
-                right = jnp.where(last_lane, bwd[(j + 1) % (T + 1)], bwd[j])
-                near = (read(j, rows_down) + read(j, rows_up)) + (right + left)
-                out.append(4.0 * c[j] - near)
-            return c, out
-
-        def row_slices(base):
-            return pl.ds(base, 8), pl.ds(base - 1, 8), pl.ds(base + 1, 8)
-
-        def store_field(f, rows, tiles, ok):
-            for j, v in enumerate(tiles):
-                if j == T:
-                    v = jnp.where(col_ok, v, 0.0)
-                if ok is not None:
-                    v = jnp.where(ok, v, 0.0)
-                V[f, j, rows, :] = v
-
-        def right_side(base, ok):
-            rows, up, down = row_slices(base)
-            labels = [L[j, rows, :] for j in range(T + 1)]
-            b = [None] * (T + 1)
-            for k in range(3):
-                _, a = stencil(lambda j, r, k=k: E[k, j, r, :], rows, up, down, T + 1)
-                b = a if k == 0 else [
-                    jnp.where(lb == k, v, w) for lb, v, w in zip(labels, a, b)]
-            store_field(0, rows, b, ok)
-
-        def apply(f, base, ok, count=T + 1):
-            rows, up, down = row_slices(base)
-            c, a = stencil(lambda j, r: V[f, j, r, :], rows, up, down, count)
-            if f < 2:
-                store_field(f + 1, rows, a, ok)
-            return c, a
+        @pl.when(has_up)
+        def _():
+            for j in range(T):
+                for k in range(3):
+                    E[k, j, 4:8, :] = RU[k, j, 4:8, :]
+                L[j, 4:8, :] = LU[j, 4:8, :]
+
+        @pl.when(has_down)
+        def _():
+            for j in range(T):
+                for k in range(3):
+                    E[k, j, 136:140, :] = RD[k, j, 0:4, :]
+                L[j, 136:140, :] = LD[j, 0:4, :]
+
+        def body(i, carry):
+            right_side_beside(pl.multiple_of(8 * i, 8))
+            return carry
+        lax.fori_loop(1, 17, body, 0, unroll=UNROLL_C)
 
         top_ok = has_up | (sub8 == 7)
         bottom_ok = has_down | (sub8 == 0)
         right_side(1, top_ok)
         right_side(135, bottom_ok)
 
-        def body(i, carry):
-            right_side(pl.multiple_of(8 * i, 8), None)
-            return carry
-        lax.fori_loop(1, 17, body, 0, unroll=UNROLL)
+        pl.semaphore_wait(known.at[1], len(two_away))
+        signal(known.at[2], at(dcore=1))
+
 
         def add_up(products):
             while len(products) > 1:
@@ -347,9 +418,9 @@
             rest = buf.at[pl.ds(0, n - 1)]
             pltpu.make_async_copy(rest, rest, red_send.at[phase]).wait()
 
+        pl.semaphore_wait(known.at[2], 1)
         reduce_start(line, red_col, 0, n_col, col, lambda p: {"row": row, "col": p})
 
-        core, x, y = row % 2, (row // 2) % X, row // (2 * X)
         w4 = weights(512, 4, 1 / 16)
         for h in range(2):
             quads = jnp.concatenate([
@@ -449,12 +520,12 @@
             q = (mine + i) % X
             late(core, q, partner, 0).wait_recv()
             late(core, q, partner, X - 1 + i).start()
-            coarse(core, q)
-        other = 1 - core
+        for i in (1, 3, 2):
+            coarse(core, (mine + i) % X)
         for i in (0, 1, 3, 2):
             q = (jnp.where(core == 0, x, y) + i) % X
-            late(other, q, partner, 0).wait_recv()
-            coarse(other, q)
+            late(1 - core, q, partner, 0).wait_recv()
+            coarse(1 - core, q)
 
         for i in range(7):
             early(0, 0, row, i).wait_send()
@@ -505,6 +576,11 @@
                 pltpu.VMEM((3, T + 1, ROWS, 128), F32),
                 pltpu.VMEM((T + 1, ROWS, 128), jnp.int32),
                 pltpu.VMEM((3, T + 1, ROWS, 128), F32),
+                pltpu.VMEM((3, ROWS, 128), F32),
+                pltpu.VMEM((3, T, 8, 128), F32),
+                pltpu.VMEM((3, T, 8, 128), F32),
+                pltpu.VMEM((T, 8, 128), jnp.int32),
+                pltpu.VMEM((T, 8, 128), jnp.int32),
                 pltpu.VMEM((2, 3, 32, 128), F32),
                 pltpu.VMEM((8, 3, 32, 128), F32),
                 pltpu.VMEM((T // 2, 3, 64, 128), F32),
@@ -524,6 +600,7 @@
                 sem((8,)),
                 sem((7,)),
                 sem((2, 4)),
+                pltpu.SemaphoreType.REGULAR((3,)),
             ],
             compiler_params=pltpu.CompilerParams(
                 collective_id=0, has_side_effects=True, vmem_limit_bytes=40 * 1024 * 1024),

time: 39.4 us -> 36.2 us (0.919)
  Pallas kernels: 38.7 us -> 35.4 us
    pallas_call x1, Pallas kernels: 37.3 us -> 34 us  [step(): pl.pallas_call(make_kernel(n_row, n_col), out_shape=(jax.ShapeDtypeStruct...]
where the time goes in v3:
time: 36.2 us; the launch traced here: 36.1 us
  Pallas kernels  35.4 us (98%)
  between operations  0.64 us (2%)
    pallas_call x1, Pallas kernels, step(): pl.pallas_call(make_kernel(n_row, n_col), out_shape=(jax.ShapeDtypeStruct...  34 us
    pallas_call x1, Pallas kernels, step(): pl.pallas_call(write_out, out_shape=(jax.ShapeDtypeStruct((128, 1024), F3...  1.41 us

profile of v3, /device:TPU:1, one launch (start us, length us, event | category | flops | bytes accessed | tf_op | source)
XLA Modules:
  0.0 36.1 jit_solution(16232553865166057142)
XLA Ops:
  0.6 34.0 %shard_map.57 = (f32[8,128,128]{2,1,0:T(8,128)S(1)}, f32[4,64,128]{2,1,0:T(8,128)S(1)}, f32[2,4,4,2,32,128]{5,4,3,2,1,0:T(8,128)S(1)}, f32[4,4,2,16,128]{4,3,2,1,0:T(8,128)S(1)}) custom-call(f32[3,128,1024]{2,1,0:T(8,128)} %src.1, s32[128,1024]{1,0:T(8,128)} %lab.1), custom_call_target="tpu_custom_call" | custom-call | tf_op jit(solution)/shard_map/pallas_call | solution.py:565
  34.7 1.4 %shard_map.58 = (f32[128,1024]{1,0:T(8,128)}, f32[64,512]{1,0:T(8,128)}, f32[4,4,2,32,256]{4,3,2,1,0:T(8,128)}, f32[4,4,2,16,128]{4,3,2,1,0:T(8,128)}) custom-call(f32[8,128,128]{2,1,0:T(8,128)S(1)} %get-tuple-element.12.O, f32[4,64,128]{2,1,0:T(8,128)S(1)} %get-tuple-element.13.FI, f32[2,4,4,2,32,128]{5,4,3,2,1,0:T(8,128)S(1)} %get-tuple-element.14.H, ...), custom_call_target="tpu_custom_call" | custom-call | tf_op jit(solution)/shard_map/pallas_call | solution.py:608

commit v4 on v3

--- a/solution.py
+++ b/solution.py
@@ -24,6 +24,11 @@
 def dd_add(a, b):
     s, e = two_sum(a[0], b[0])
     return two_sum(s, e + (a[1] + b[1]))
+
+
+def pair_add(a, b):
+    s, e = two_sum(a[0], b[0])
+    return s, (a[1] + b[1]) + e
 
 
 def dd_neg(a):
@@ -168,6 +173,10 @@
         def to(r, c):
             return dict(device_id={"row": r, "col": c}, device_id_type=MESH)
 
+        for device in beside_us:
+            signal(known.at[0], device)
+
+
         halo = []
 
         def exchange(slot, s_ref, d_ref, goes, r, c, comes):
@@ -180,8 +189,6 @@
                 cp.start()
             halo.append((cp, goes, comes))
 
-        exchange(0, strip, strip_in.at[0], has_right, row, col + 1, has_left)
-        exchange(1, strip, strip_in.at[1], has_left, row, col - 1, has_right)
         first4, last4 = pl.ds(8, 4), pl.ds(132, 4)
         exchange(2, E.at[:, pl.ds(0, T), first4, :], RD.at[:, :, pl.ds(0, 4), :],
                  has_up, row - 1, col, has_down)
@@ -194,13 +201,15 @@
         slot = 6
         opposite = (diagonal[3][2], diagonal[2][2], diagonal[1][2], diagonal[0][2])
         for q, (dr, dc, there) in enumerate(diagonal):
-            rows = pl.ds(8 if dr < 0 else 128, 8)
-            j = 0 if dc < 0 else T - 1
+            rows, j = pl.ds(8 if dr < 0 else 128, 8), 0 if dc < 0 else T - 1
             exchange(slot, E.at[:, j, rows, :], corner_in.at[q], there, row + dr, col + dc,
                      opposite[q])
             exchange(slot + 1, L.at[j, rows, :], corner_lab.at[q], there, row + dr, col + dc,
                      opposite[q])
             slot += 2
+
+        exchange(0, strip, strip_in.at[0], has_right, row, col + 1, has_left)
+        exchange(1, strip, strip_in.at[1], has_left, row, col - 1, has_right)
 
         lane8 = lax.broadcasted_iota(jnp.int32, (8, 128), 1)
         sub8 = lax.broadcasted_iota(jnp.int32, (8, 128), 0)
@@ -285,20 +294,56 @@
             V[0, T - 1, rows, :] = V[0, T - 1, rows, :] - jnp.where(
                 last_lane, choose(L[T - 1, rows, :], bwd), 0.0)
 
-        for device in beside_us:
-            signal(known.at[0], device)
-
         def body(i, carry):
             right_side_alone(pl.multiple_of(8 * i, 8))
             return carry
-        lax.fori_loop(1, 17, body, 0, unroll=UNROLL_B)
-
+        lax.fori_loop(1, 9, body, 0, unroll=UNROLL_B)
         pl.semaphore_wait(known.at[0], len(beside_us))
         two_away = [at(dx=2), at(dy=2), at(dcol=2), at(dcol=-2)]
         for device in two_away:
             signal(known.at[1], device)
-
-        for cp, goes, comes in halo:
+        lax.fori_loop(9, 17, body, 0, unroll=UNROLL_B)
+
+        def add_up(products):
+            while len(products) > 1:
+                odd = products[-1:] if len(products) % 2 else []
+                products = [a + b for a, b in zip(products[::2], products[1::2])] + odd
+            return products[0]
+
+        zero8 = jnp.zeros((8, 128), F32)
+
+        def alone(f, base, inner):
+            rows, up, down = row_slices(base)
+            c = [V[f, j, rows, :] for j in range(T)]
+            fwd = [pltpu.roll(v, 1, axis=1) for v in c]
+            bwd = [pltpu.roll(v, 127, axis=1) for v in c]
+            a = []
+            for j in range(T):
+                left = jnp.where(first_lane, fwd[j - 1] if j else 0.0, fwd[j])
+                right = jnp.where(last_lane, bwd[j + 1] if j < T - 1 else 0.0, bwd[j])
+                near = (V[f, j, down, :] + V[f, j, up, :]) + (right + left)
+                a.append(4.0 * c[j] - near)
+                if f < 2:
+                    V[f + 1, j, rows, :] = a[j]
+            if inner:
+                return (add_up([c[j] * c[j] for j in range(1, T - 1)]),
+                        add_up([c[j] * a[j] for j in range(1, T - 1)]))
+
+        sums = []
+        for f in range(3):
+            V[f, 0:T, 0:8, :] = jnp.zeros((T, 8, 128), F32)
+            V[f, 0:T, 136:144, :] = jnp.zeros((T, 8, 128), F32)
+            if f < 2:
+                alone(f, 8, False)
+                alone(f, 128, False)
+
+            def body(i, carry, f=f):
+                got = alone(f, pl.multiple_of(8 * i, 8), True)
+                return carry[0] + got[0], carry[1] + got[1]
+            sums += list(lax.fori_loop(2, 16, body, (zero8, zero8), unroll=14))
+
+        strips, halo = halo[-2:], halo[:-2]
+        for cp, goes, comes in strips:
             @pl.when(comes)
             def _(cp=cp):
                 cp.wait_recv()
@@ -315,6 +360,16 @@
             else:
                 L[T, 8:136, :] = tile.astype(jnp.int32)
 
+        def body(i, carry):
+            right_side_beside(pl.multiple_of(8 * i, 8))
+            return carry
+        lax.fori_loop(1, 17, body, 0, unroll=UNROLL_C)
+
+        for cp, goes, comes in halo:
+            @pl.when(comes)
+            def _(cp=cp):
+                cp.wait_recv()
+
         for rows, from_left, from_right in ((slice(0, 8), 3, 2), (slice(136, 144), 1, 0)):
             l_ok, r_ok = opposite[from_left], opposite[from_right]
             for k in range(3):
@@ -339,48 +394,59 @@
                     E[k, j, 136:140, :] = RD[k, j, 0:4, :]
                 L[j, 136:140, :] = LD[j, 0:4, :]
 
-        def body(i, carry):
-            right_side_beside(pl.multiple_of(8 * i, 8))
-            return carry
-        lax.fori_loop(1, 17, body, 0, unroll=UNROLL_C)
-
         top_ok = has_up | (sub8 == 7)
         bottom_ok = has_down | (sub8 == 0)
         right_side(1, top_ok)
         right_side(135, bottom_ok)
 
-        pl.semaphore_wait(known.at[1], len(two_away))
-        signal(known.at[2], at(dcore=1))
-
-
-        def add_up(products):
-            while len(products) > 1:
-                products = [a + b for a, b in zip(products[::2], products[1::2])]
-            return products[0]
-
-        zero8 = jnp.zeros((8, 128), F32)
-        sums = []
+        def rim(f, base):
+            rows, up, down = row_slices(base)
+            c = {j: V[f, j, rows, :] for j in (T - 2, T - 1, T, 0, 1)}
+            fwd = {j: pltpu.roll(c[j], 1, axis=1) for j in (T - 2, T - 1, T, 0)}
+            bwd = {j: pltpu.roll(c[j], 127, axis=1) for j in (T - 1, T, 0, 1)}
+            a = {}
+            for before, j, after in ((T - 2, T - 1, T), (T - 1, T, 0), (T, 0, 1)):
+                if j == T and f == 2:
+                    continue
+                left = jnp.where(first_lane, fwd[before], fwd[j])
+                right = jnp.where(last_lane, bwd[after], bwd[j])
+                near = (V[f, j, down, :] + V[f, j, up, :]) + (right + left)
+                a[j] = 4.0 * c[j] - near
+                if f < 2:
+                    V[f + 1, j, rows, :] = jnp.where(col_ok, a[j], 0.0) if j == T else a[j]
+            return c[0] * c[0] + c[T - 1] * c[T - 1], c[0] * a[0] + c[T - 1] * a[T - 1]
+
         for f in range(3):
             if f < 2:
                 apply(f, 1, top_ok)
                 apply(f, 135, bottom_ok)
+            same, next_ = sums[2 * f], sums[2 * f + 1]
+            for base in (8, 128):
+                c, a = apply(f, base, None, T + 1 if f < 2 else T)
+                same = same + add_up([c[j] * c[j] for j in range(T)])
+                next_ = next_ + add_up([c[j] * a[j] for j in range(T)])
 
             def body(i, carry, f=f):
-                c, a = apply(f, pl.multiple_of(8 * i, 8), None, T + 1 if f < 2 else T)
-                same = add_up([c[j] * c[j] for j in range(T)])
-                next_ = add_up([c[j] * a[j] for j in range(T)])
-                return carry[0] + same, carry[1] + next_
-            sums += list(lax.fori_loop(1, 17, body, (zero8, zero8), unroll=UNROLL))
+                got = rim(f, pl.multiple_of(8 * i, 8))
+                return carry[0] + got[0], carry[1] + got[1]
+            sums[2 * f:2 * f + 2] = lax.fori_loop(2, 16, body, (same, next_), unroll=14)
 
         pairs = [(s, zero8) for s in sums]
         for shift in (4, 2, 1):
-            pairs = [dd_add(p, (pltpu.roll(p[0], shift, axis=0), pltpu.roll(p[1], shift, axis=0)))
+            pairs = [pair_add(p, (pltpu.roll(p[0], shift, axis=0), pltpu.roll(p[1], shift, axis=0)))
                      for p in pairs]
         hi, lo = zero8, zero8
         for m, p in enumerate(pairs):
             hi, lo = jnp.where(sub8 == m, p[0], hi), jnp.where(sub8 == m, p[1], lo)
-        for shift in (64, 32, 16, 8, 4, 2, 1):
-            hi, lo = dd_add((hi, lo), (pltpu.roll(hi, shift, axis=1), pltpu.roll(lo, shift, axis=1)))
+        top = hi.astype(jnp.bfloat16).astype(F32)
+        mid = (hi - top).astype(jnp.bfloat16).astype(F32)
+        low = (hi - top) - mid
+        lo_top = lo.astype(jnp.bfloat16).astype(F32)
+        pieces = jnp.concatenate([top, mid, low, lo_top, lo - lo_top], axis=0)
+        added = jnp.dot(pieces.astype(jnp.bfloat16), jnp.ones((128, 128), jnp.bfloat16),
+                        preferred_element_type=F32).reshape(5, 8, 128)
+        hi, lo = two_sum(added[0], added[1])
+        hi, lo = two_sum(hi, lo + (added[2] + (added[3] + added[4])))
         line = jnp.where(lane8 == sub8, hi, 0.0) + jnp.where(lane8 == sub8 + 8, lo, 0.0)
         line = jnp.sum(line, axis=0, keepdims=True)
 
@@ -398,15 +464,14 @@
             return jnp.where(lane1 < 8, h, 0.0) + jnp.where(
                 (lane1 >= 8) & (lane1 < 16), pltpu.roll(l, 8, axis=1), 0.0)
 
-        def reduce_start(line, buf, phase, n, me, device):
+        def reduce_start(line, buf, phase, me, peers):
             msg[phase] = line
             buf[me] = line
 
-            @pl.loop(1, n)
-            def _(i):
+            for device in peers:
                 pltpu.make_async_remote_copy(
                     src_ref=msg.at[phase], dst_ref=buf.at[me], send_sem=red_send.at[phase],
-                    recv_sem=red_recv.at[phase], device_id=device((me + i) % n),
+                    recv_sem=red_recv.at[phase], device_id=device,
                     device_id_type=MESH).start()
 
         def reduce_end(buf, phase, n):
@@ -418,8 +483,10 @@
             rest = buf.at[pl.ds(0, n - 1)]
             pltpu.make_async_copy(rest, rest, red_send.at[phase]).wait()
 
-        pl.semaphore_wait(known.at[2], 1)
-        reduce_start(line, red_col, 0, n_col, col, lambda p: {"row": row, "col": p})
+        pl.semaphore_wait(known.at[1], len(two_away))
+        signal(known.at[2], at(dcore=1))
+        reduce_start(line, red_col, 0, col, [
+            at(dcol=d) for d in sorted(range(1, n_col), key=lambda d: -min(d, n_col - d))])
 
         w4 = weights(512, 4, 1 / 16)
         for h in range(2):
@@ -435,6 +502,7 @@
                 src_ref=MB.at[h], dst_ref=PB.at[slot], send_sem=p_send.at[sem],
                 recv_sem=p_recv.at[slot], **to(peer, col))
 
+        pl.semaphore_wait(known.at[2], 1)
         early(1 - core, 2 * jnp.where(core == 0, y, x) + core, row + 1 - 2 * core, 0).start()
         for i in range(1, X):
             early(0, 2 * x + core, (y * X + (x + i) % X) * 2, i).start()
@@ -454,7 +522,10 @@
         fine_part(0)
         fine_part(1)
         line = reduce_end(red_col, 0, n_col)
-        reduce_start(line, red_row, 1, n_row, row, lambda p: {"row": p, "col": col})
+        reduce_start(line, red_row, 1, row, [
+            at(dx=dx, dy=dy, dcore=c) for dx, dy, c in sorted(
+                [(dx, dy, c) for dx in range(X) for dy in range(n_y) for c in range(2)][1:],
+                key=lambda d: -min(d[0], X - d[0]) - min(d[1], n_y - d[1]) - d[2] / 2)])
         fine_part(2)
         fine_part(3)
         CO[...] = jnp.zeros((n_y, X, 2, 16, 128), F32)
@@ -532,7 +603,7 @@
         for i in range(7):
             late(0, 0, row, i).wait_send()
         reduce_sent(red_row, 1, n_row)
-        for cp, goes, comes in halo:
+        for cp, goes, comes in halo + strips:
             @pl.when(goes)
             def _(cp=cp):
                 cp.wait_send()
@@ -541,10 +612,10 @@
 
 
 def write_out(O, FI, H, CO, o_blend, o_fine, o_mid, o_coarse, sem):
-    copies = [(H.at[0], o_mid.at[:, :, :, :, pl.ds(0, 128)])]
+    copies = [(H.at[0, q], o_mid.at[q, :, :, :, pl.ds(0, 128)]) for q in range(X)]
     copies += [(H.at[1, q], o_mid.at[:, q, :, :, pl.ds(128, 128)]) for q in range(X)]
     copies += [(O.at[j], o_blend.at[:, pl.ds(128 * j, 128)]) for j in range(T)]
-    copies += [(CO, o_coarse)]
+    copies += [(CO.at[q], o_coarse.at[q]) for q in range(CO.shape[0])]
     copies += [(FI.at[j], o_fine.at[:, pl.ds(128 * j, 128)]) for j in range(T // 2)]
     copies = [pltpu.make_async_copy(a, b, sem.at[i]) for i, (a, b) in enumerate(copies)]
     for cp in copies:
@@ -615,7 +686,7 @@
             ),
             in_specs=[vmem] * 4,
             out_specs=(hbm,) * 4,
-            scratch_shapes=[sem((5 + T + 1 + T // 2,))],
+            scratch_shapes=[sem((2 * X + T + n_y + T // 2,))],
             compiler_params=pltpu.CompilerParams(vmem_limit_bytes=1024 * 1024),
         )(*parts)
         return blended, fine, mid.reshape(-1, 256), coarse.reshape(-1, 128)

time: 36.2 us -> 35.1 us (0.970)
  Pallas kernels: 35.4 us -> 34.3 us
    pallas_call x1, Pallas kernels: 34 us -> 32.9 us  [step(): pl.pallas_call(make_kernel(n_row, n_col), out_shape=(jax.ShapeDtypeStruct...]
where the time goes in v4:
time: 35.1 us; the launch traced here: 35 us
  Pallas kernels  34.3 us (98%)
  between operations  0.64 us (2%)
    pallas_call x1, Pallas kernels, step(): pl.pallas_call(make_kernel(n_row, n_col), out_shape=(jax.ShapeDtypeStruct...  32.9 us
    pallas_call x1, Pallas kernels, step(): pl.pallas_call(write_out, out_shape=(jax.ShapeDtypeStruct((128, 1024), F3...  1.46 us

profile of v4, /device:TPU:1, one launch (start us, length us, event | category | flops | bytes accessed | tf_op | source)
XLA Modules:
  0.0 35.0 jit_solution(9454995999224154732)
XLA Ops:
  0.6 32.9 %shard_map.57 = (f32[8,128,128]{2,1,0:T(8,128)S(1)}, f32[4,64,128]{2,1,0:T(8,128)S(1)}, f32[2,4,4,2,32,128]{5,4,3,2,1,0:T(8,128)S(1)}, f32[4,4,2,16,128]{4,3,2,1,0:T(8,128)S(1)}) custom-call(f32[3,128,1024]{2,1,0:T(8,128)} %src.1, s32[128,1024]{1,0:T(8,128)} %lab.1), custom_call_target="tpu_custom_call" | custom-call | tf_op jit(solution)/shard_map/pallas_call | solution.py:636
  33.5 1.5 %shard_map.58 = (f32[128,1024]{1,0:T(8,128)}, f32[64,512]{1,0:T(8,128)}, f32[4,4,2,32,256]{4,3,2,1,0:T(8,128)}, f32[4,4,2,16,128]{4,3,2,1,0:T(8,128)}) custom-call(f32[8,128,128]{2,1,0:T(8,128)S(1)} %get-tuple-element.12.O, f32[4,64,128]{2,1,0:T(8,128)S(1)} %get-tuple-element.13.FI, f32[2,4,4,2,32,128]{5,4,3,2,1,0:T(8,128)S(1)} %get-tuple-element.14.H, ...), custom_call_target="tpu_custom_call" | custom-call | tf_op jit(solution)/shard_map/pallas_call | solution.py:679

commit v5 on v4

--- a/solution.py
+++ b/solution.py
@@ -11,8 +11,8 @@
 ROWS = 144
 X = 4
 UNROLL = 16
-UNROLL_B = 4
-UNROLL_C = 8
+UNROLL_B = 8
+UNROLL_C = 16
 
 
 def two_sum(a, b):
@@ -131,22 +131,22 @@
 
         barrier = pltpu.get_barrier_semaphore()
         beside_us = [at(dcore=1), at(dx=1), at(dx=-1), at(dy=1), at(dy=-1), at(dcol=1), at(dcol=-1)]
-        for device in beside_us:
-            signal(barrier, device)
         step = 2 * core - 1
         cross = jnp.where(core == 1, has_down, has_up)
         diagonal = ((-1, -1, has_up & has_left), (-1, 1, has_up & has_right),
                     (1, -1, has_down & has_left), (1, 1, has_down & has_right))
         expected = len(beside_us) + cross.astype(jnp.int32)
 
-        @pl.when(cross)
-        def _():
-            signal(barrier, {"row": row + step, "col": col})
         for dr, dc, there in diagonal:
             @pl.when(there)
             def _(dr=dr, dc=dc):
                 signal(barrier, {"row": row + dr, "col": col + dc})
             expected = expected + there.astype(jnp.int32)
+        @pl.when(cross)
+        def _():
+            signal(barrier, {"row": row + step, "col": col})
+        for device in beside_us:
+            signal(barrier, device)
 
         for rows in (slice(0, 8), slice(136, 144)):
             E[:, 0:T, rows, :] = jnp.zeros((3, T, 8, 128), F32)
@@ -189,6 +189,8 @@
                 cp.start()
             halo.append((cp, goes, comes))
 
+        exchange(0, strip, strip_in.at[0], has_right, row, col + 1, has_left)
+        exchange(1, strip, strip_in.at[1], has_left, row, col - 1, has_right)
         first4, last4 = pl.ds(8, 4), pl.ds(132, 4)
         exchange(2, E.at[:, pl.ds(0, T), first4, :], RD.at[:, :, pl.ds(0, 4), :],
                  has_up, row - 1, col, has_down)
@@ -208,9 +210,6 @@
                      opposite[q])
             slot += 2
 
-        exchange(0, strip, strip_in.at[0], has_right, row, col + 1, has_left)
-        exchange(1, strip, strip_in.at[1], has_left, row, col - 1, has_right)
-
         lane8 = lax.broadcasted_iota(jnp.int32, (8, 128), 1)
         sub8 = lax.broadcasted_iota(jnp.int32, (8, 128), 0)
         low4, high4 = lane8 < 4, lane8 >= 124
@@ -297,12 +296,7 @@
         def body(i, carry):
             right_side_alone(pl.multiple_of(8 * i, 8))
             return carry
-        lax.fori_loop(1, 9, body, 0, unroll=UNROLL_B)
-        pl.semaphore_wait(known.at[0], len(beside_us))
-        two_away = [at(dx=2), at(dy=2), at(dcol=2), at(dcol=-2)]
-        for device in two_away:
-            signal(known.at[1], device)
-        lax.fori_loop(9, 17, body, 0, unroll=UNROLL_B)
+        lax.fori_loop(1, 17, body, 0, unroll=UNROLL_B)
 
         def add_up(products):
             while len(products) > 1:
@@ -341,8 +335,13 @@
                 got = alone(f, pl.multiple_of(8 * i, 8), True)
                 return carry[0] + got[0], carry[1] + got[1]
             sums += list(lax.fori_loop(2, 16, body, (zero8, zero8), unroll=14))
-
-        strips, halo = halo[-2:], halo[:-2]
+            if f == 0:
+                pl.semaphore_wait(known.at[0], len(beside_us))
+                two_away = [at(dx=2), at(dy=2), at(dcol=2), at(dcol=-2)]
+                for device in two_away:
+                    signal(known.at[1], device)
+
+        strips, halo = halo[:2], halo[2:]
         for cp, goes, comes in strips:
             @pl.when(comes)
             def _(cp=cp):

time: 35.1 us -> 34.7 us (0.989)
  Pallas kernels: 34.3 us -> 33.9 us
    pallas_call x1, Pallas kernels: 32.9 us -> 32.5 us  [step(): pl.pallas_call(make_kernel(n_row, n_col), out_shape=(jax.ShapeDtypeStruct...]
where the time goes in v5:
time: 34.7 us; the launch traced here: 34.6 us
  Pallas kernels  33.9 us (98%)
  between operations  0.64 us (2%)
    pallas_call x1, Pallas kernels, step(): pl.pallas_call(make_kernel(n_row, n_col), out_shape=(jax.ShapeDtypeStruct...  32.5 us
    pallas_call x1, Pallas kernels, step(): pl.pallas_call(write_out, out_shape=(jax.ShapeDtypeStruct((128, 1024), F3...  1.46 us

profile of v5, /device:TPU:1, one launch (start us, length us, event | category | flops | bytes accessed | tf_op | source)
XLA Modules:
  0.0 34.6 jit_solution(15091735066271224081)
XLA Ops:
  0.6 32.5 %shard_map.57 = (f32[8,128,128]{2,1,0:T(8,128)S(1)}, f32[4,64,128]{2,1,0:T(8,128)S(1)}, f32[2,4,4,2,32,128]{5,4,3,2,1,0:T(8,128)S(1)}, f32[4,4,2,16,128]{4,3,2,1,0:T(8,128)S(1)}) custom-call(f32[3,128,1024]{2,1,0:T(8,128)} %src.1, s32[128,1024]{1,0:T(8,128)} %lab.1), custom_call_target="tpu_custom_call" | custom-call | tf_op jit(solution)/shard_map/pallas_call | solution.py:635
  33.1 1.5 %shard_map.58 = (f32[128,1024]{1,0:T(8,128)}, f32[64,512]{1,0:T(8,128)}, f32[4,4,2,32,256]{4,3,2,1,0:T(8,128)}, f32[4,4,2,16,128]{4,3,2,1,0:T(8,128)}) custom-call(f32[8,128,128]{2,1,0:T(8,128)S(1)} %get-tuple-element.12.O, f32[4,64,128]{2,1,0:T(8,128)S(1)} %get-tuple-element.13.FI, f32[2,4,4,2,32,128]{5,4,3,2,1,0:T(8,128)S(1)} %get-tuple-element.14.H, ...), custom_call_target="tpu_custom_call" | custom-call | tf_op jit(solution)/shard_map/pallas_call | solution.py:678

commit v6 on v5

--- a/solution.py
+++ b/solution.py
@@ -586,6 +586,14 @@
                 CO[at] = CO[at] + out[16 * s:16 * s + 16, :]
 
         coarse(core, mine)
+        for i in range(7):
+            early(0, 0, row, i).wait_send()
+        reduce_sent(red_row, 1, n_row)
+        for cp, goes, comes in halo + strips:
+            @pl.when(goes)
+            def _(cp=cp):
+                cp.wait_send()
+
         for i in (1, 3, 2):
             q = (mine + i) % X
             late(core, q, partner, 0).wait_recv()
@@ -598,14 +606,7 @@
             coarse(1 - core, q)
 
         for i in range(7):
-            early(0, 0, row, i).wait_send()
-        for i in range(7):
             late(0, 0, row, i).wait_send()
-        reduce_sent(red_row, 1, n_row)
-        for cp, goes, comes in halo + strips:
-            @pl.when(goes)
-            def _(cp=cp):
-                cp.wait_send()
 
     return kernel
 

time: 34.7 us -> 34.7 us (level)
  no operation moved by 1% of the time
where the time goes in v6:
time: 34.7 us; the launch traced here: 34.6 us
  Pallas kernels  33.9 us (98%)
  between operations  0.64 us (2%)
    pallas_call x1, Pallas kernels, step(): pl.pallas_call(make_kernel(n_row, n_col), out_shape=(jax.ShapeDtypeStruct...  32.5 us
    pallas_call x1, Pallas kernels, step(): pl.pallas_call(write_out, out_shape=(jax.ShapeDtypeStruct((128, 1024), F3...  1.46 us

profile of v6, /device:TPU:1, one launch (start us, length us, event | category | flops | bytes accessed | tf_op | source)
XLA Modules:
  0.0 34.6 jit_solution(13461571967061564002)
XLA Ops:
  0.6 32.5 %shard_map.57 = (f32[8,128,128]{2,1,0:T(8,128)S(1)}, f32[4,64,128]{2,1,0:T(8,128)S(1)}, f32[2,4,4,2,32,128]{5,4,3,2,1,0:T(8,128)S(1)}, f32[4,4,2,16,128]{4,3,2,1,0:T(8,128)S(1)}) custom-call(f32[3,128,1024]{2,1,0:T(8,128)} %src.1, s32[128,1024]{1,0:T(8,128)} %lab.1), custom_call_target="tpu_custom_call" | custom-call | tf_op jit(solution)/shard_map/pallas_call | solution.py:636
  33.1 1.5 %shard_map.58 = (f32[128,1024]{1,0:T(8,128)}, f32[64,512]{1,0:T(8,128)}, f32[4,4,2,32,256]{4,3,2,1,0:T(8,128)}, f32[4,4,2,16,128]{4,3,2,1,0:T(8,128)}) custom-call(f32[8,128,128]{2,1,0:T(8,128)S(1)} %get-tuple-element.12.O, f32[4,64,128]{2,1,0:T(8,128)S(1)} %get-tuple-element.13.FI, f32[2,4,4,2,32,128]{5,4,3,2,1,0:T(8,128)S(1)} %get-tuple-element.14.H, ...), custom_call_target="tpu_custom_call" | custom-call | tf_op jit(solution)/shard_map/pallas_call | solution.py:679
